TPU v7x, 768 devices: a whole 4x8x12 slice. The times are simulated.
768 devices in a mesh: ta: 48 (over y, z_lo, core), gz: 16 (over x, z_hi).
Axes of the slice: x: 4, y: 8, z: 12 (z_hi: 4, z_lo: 3; z = z_hi * 3 + z_lo), core: 2. Of those that a mesh axis runs over, the one named last changes fastest.
Arguments:
- source: bfloat16 [48, 16, 2, 4, 3, 12, 256], P('ta', 'gz'), may hold values from -6 to 6
- gauge_field: bfloat16 [48, 16, 4, 2, 3, 3, 256], P('ta', 'gz'), may hold values from -2.5 to 2.5
Outputs:
- twice_applied: bfloat16 [48, 16, 2, 4, 3, 12, 256], P('ta', 'gz')
All inputs are finite; a program needn't handle non-finite values.
Results may differ from a plain program's by a relative error of at most 0.0075.
Values may be sent and summed in bfloat16 or wider, within the bound.
No kernel may reach another device: no remote copies, remote signals or barrier semaphores. Data moves between devices by JAX's collectives and lax.ppermute only.
A program may use at most 64 MiB of HBM per device.

v0:
```python
import jax
import jax.numpy as jnp
from jax import lax
from jax.experimental import pallas as pl
from jax.experimental.pallas import tpu as pltpu
from jax.sharding import PartitionSpec as P

HOPPING = 0.124
F32 = jnp.float32
BF16 = jnp.bfloat16
LANES = 128


def lane_iota():
    return lax.broadcasted_iota(jnp.int32, (8, LANES), 1)


def row_iota():
    return lax.broadcasted_iota(jnp.int32, (8, LANES), 0)


def get(ref, k, r, j):
    return ref[k, r * 8 : r * 8 + 8, j * LANES : (j + 1) * LANES].astype(F32)


def links(u_ref, mu, j):
    def one(a, b, ri):
        row = ((mu * 3 + a) * 3 + b) * 2 + ri
        return jnp.broadcast_to(u_ref[row : row + 1, j * LANES : (j + 1) * LANES], (8, LANES))

    return [[(one(a, b, 0), one(a, b, 1)) for b in range(3)] for a in range(3)]


def times(u, h, adjoint):
    re, im = [], []
    for a in range(3):
        total_re = total_im = None
        for b in range(3):
            if adjoint:
                ur, ui = u[b][a]
                tr = ur * h[b] + ui * h[3 + b]
                ti = ur * h[3 + b] - ui * h[b]
            else:
                ur, ui = u[a][b]
                tr = ur * h[b] - ui * h[3 + b]
                ti = ur * h[3 + b] + ui * h[b]
            total_re = tr if total_re is None else total_re + tr
            total_im = ti if total_im is None else total_im + ti
        re.append(total_re)
        im.append(total_im)
    return re + im


def row_sign(r, value):
    if r == 0:
        return value
    if r == 2:
        return -value
    return jnp.where(row_iota() < 4, value, -value)


def swap_spins(tiles):
    turned = [pltpu.roll(t, 4, 0) for t in tiles]
    low = row_iota() < 4
    return [jnp.where(low, turned[(i + 1) % 3], turned[(i + 2) % 3]) for i in range(3)]


def mix(mu, r, up, dn, q):
    out = []
    for k in range(6):
        if mu in (0, 2):
            other = dn[k + 3] if k < 3 else dn[k - 3]
            other = other if k < 3 else -other
        else:
            other = -dn[k]
        if mu == 1:
            other = row_sign(r, -other)
        elif mu == 2:
            other = row_sign(r, other)
        out.append(up[k] + other if q > 0 else up[k] - other)
    return out


def spread(mu, r, k6, q):
    out = []
    for k in range(6):
        if mu in (0, 2):
            value = -k6[k + 3] if k < 3 else k6[k - 3]
        else:
            value = -k6[k]
        if mu == 1:
            value = row_sign(r, -value)
        elif mu == 2:
            value = row_sign(r, value)
        out.append(value if q > 0 else -value)
    return out


def shift_x(tile, ahead):
    x = lane_iota() & 15
    if ahead:
        return jnp.where(x == 15, pltpu.roll(tile, 15, 1), pltpu.roll(tile, 127, 1))
    return jnp.where(x == 0, pltpu.roll(tile, 113, 1), pltpu.roll(tile, 1, 1))


def shift_y(pair, ahead):
    lane = lane_iota()
    if ahead:
        a, b = (pltpu.roll(t, 112, 1) for t in pair)
        inside = lane < 112
    else:
        a, b = (pltpu.roll(t, 16, 1) for t in pair)
        inside = lane >= 16
    return [jnp.where(inside, a, b), jnp.where(inside, b, a)]


def project_edges(field, u_ref, flag_ref, z_one, z_two, t_near, t_far):
    odd = flag_ref[0] > 0.5
    for j in range(2):
        for mu, first, second in ((2, z_one, z_two), (3, t_near, t_far)):
            u = links(u_ref, mu, j)
            for r in range(3):
                up = [field(k, r, j) for k in range(6)]
                dn = [field(k, r + 3, j) for k in range(6)]
                fwd = mix(mu, r, up, dn, 1)
                bwd = times(u, mix(mu, r, up, dn, -1), True)
                if mu == 3:
                    fwd = [v * flag_ref[1] for v in fwd]
                    bwd = [v * flag_ref[2] for v in bwd]
                for k in range(6):
                    at = (k, slice(r * 8, r * 8 + 8), slice(j * LANES, (j + 1) * LANES))
                    first[at] = jnp.where(odd, fwd[k], bwd[k]).astype(BF16)
                    second[at] = jnp.where(odd, bwd[k], fwd[k]).astype(BF16)


def first_edges(flag_ref, f_ref, u_ref, z_one, z_two, t_near, t_far):
    project_edges(lambda k, r, j: get(f_ref, k, r, j), u_ref, flag_ref, z_one, z_two, t_near, t_far)


def space_hops(f_ref, u_ref, acc_ref):
    up_acc = {}
    dn_acc = {}

    def add(r, j, mu, k6, q):
        low = spread(mu, r, k6, q)
        for k in range(6):
            key = (k, r, j)
            up_acc[key] = k6[k] if key not in up_acc else up_acc[key] + k6[k]
            dn_acc[key] = low[k] if key not in dn_acc else dn_acc[key] + low[k]

    swapped = {}
    for j in range(2):
        for k in range(6):
            for r, tile in enumerate(swap_spins([get(f_ref, k, 3 + i, j) for i in range(3)])):
                swapped[k, r, j] = tile
    for r in range(3):
        up = [[get(f_ref, k, r, j) for k in range(6)] for j in range(2)]
        dn = [[swapped[k, r, j] for k in range(6)] for j in range(2)]
        for j in range(2):
            u = links(u_ref, 0, j)
            ahead = [shift_x(v, True) for v in mix(0, r, up[j], dn[j], 1)]
            add(r, j, 0, times(u, ahead, False), 1)
            behind = [shift_x(v, False) for v in times(u, mix(0, r, up[j], dn[j], -1), True)]
            add(r, j, 0, behind, -1)
        us = [links(u_ref, 1, j) for j in range(2)]
        half = [mix(1, r, up[j], dn[j], 1) for j in range(2)]
        moved = [shift_y([half[0][k], half[1][k]], True) for k in range(6)]
        for j in range(2):
            add(r, j, 1, times(us[j], [moved[k][j] for k in range(6)], False), 1)
        half = [times(us[j], mix(1, r, up[j], dn[j], -1), True) for j in range(2)]
        moved = [shift_y([half[0][k], half[1][k]], False) for k in range(6)]
        for j in range(2):
            add(r, j, 1, [moved[k][j] for k in range(6)], -1)
        for j in range(2):
            for k in range(6):
                lanes = slice(j * LANES, (j + 1) * LANES)
                acc_ref[k, r * 8 : r * 8 + 8, lanes] = up_acc.pop((k, r, j))
                acc_ref[k, 24 + r * 8 : 32 + r * 8, lanes] = dn_acc.pop((k, r, j))


def finish(flag_ref, f_ref, u_ref, acc_ref, z_one, z_two, t_near, t_far, out_ref):
    odd = flag_ref[0] > 0.5
    for j in range(2):
        lanes = slice(j * LANES, (j + 1) * LANES)
        uz = links(u_ref, 2, j)
        ut = links(u_ref, 3, j)
        low = [swap_spins([get(acc_ref, k, 3 + i, j) for i in range(3)]) for k in range(6)]
        for r in range(3):
            up = [get(acc_ref, k, r, j) for k in range(6)]
            dn = [low[k][r] for k in range(6)]
            one = [get(z_one, k, r, j) for k in range(6)]
            two = [get(z_two, k, r, j) for k in range(6)]
            near = [get(t_near, k, r, j) for k in range(6)]
            far = [get(t_far, k, r, j) for k in range(6)]
            parts = (
                (2, times(uz, [jnp.where(odd, a, b) for a, b in zip(one, two)], False), 1),
                (2, [jnp.where(odd, b, a) for a, b in zip(one, two)], -1),
                (3, times(ut, [jnp.where(odd, b, a) for a, b in zip(near, far)], False), 1),
                (3, [jnp.where(odd, a, b) for a, b in zip(near, far)], -1),
            )
            for mu, k6, q in parts:
                lower = spread(mu, r, k6, q)
                up = [a + b for a, b in zip(up, k6)]
                dn = [a + b for a, b in zip(dn, lower)]
            for k in range(6):
                for at, hop in ((r, up[k]), (r + 3, dn[k])):
                    value = get(f_ref, k, at, j) - HOPPING * hop
                    out_ref[k, at * 8 : at * 8 + 8, lanes] = value.astype(BF16)


def finish_and_edges(flag_ref, f_ref, u_ref, acc_ref, z1, z2, t1, t2, out_ref, z_one, z_two, t_near, t_far):
    finish(flag_ref, f_ref, u_ref, acc_ref, z1, z2, t1, t2, out_ref)
    project_edges(lambda k, r, j: get(out_ref, k, r, j), u_ref, flag_ref, z_one, z_two, t_near, t_far)


SPINOR = pltpu.VMEM((6, 48, 256), BF16)
HALF = pltpu.VMEM((6, 24, 256), BF16)
SUM = pltpu.VMEM((6, 48, 256), F32)


def call(kernel, name, outs, flags, *args):
    in_vmem = pl.BlockSpec(memory_space=pltpu.VMEM)
    specs = [in_vmem] * len(args)
    args = tuple(pltpu.with_memory_space_constraint(a, pltpu.VMEM) for a in args)
    given = args
    if flags is not None:
        specs = [pl.BlockSpec(memory_space=pltpu.SMEM)] + specs
        given = (flags,) + args
    return pl.pallas_call(
        kernel,
        out_shape=outs,
        in_specs=specs,
        out_specs=[in_vmem] * len(outs) if isinstance(outs, list) else in_vmem,
        name=name,
    )(*given)


def routes(nt, nz):
    z_one, z_two, t_near, t_far = [], [], [], []
    for t in range(nt):
        for z in range(nz):
            here = t * nz + z
            ahead, behind = t * nz + (z + 1) % nz, t * nz + (z - 1) % nz
            later, earlier = (t + 1) % nt * nz + z, (t - 1) % nt * nz + z
            odd = t % 2
            z_one.append((here, behind if odd else ahead))
            z_two.append((here, ahead if odd else behind))
            t_near.append((here, earlier if odd else later))
            t_far.append((here, later if odd else earlier))
    return z_one, z_two, t_near, t_far


def body(source, gauge_field):
    nt, nz = lax.axis_size("ta"), lax.axis_size("gz")
    ta = lax.axis_index("ta")
    flags = jnp.stack(
        [
            (ta % 2).astype(F32),
            jnp.where(ta == 0, -1.0, 1.0).astype(F32),
            jnp.where(ta == nt - 1, -1.0, 1.0).astype(F32),
        ]
    )
    field = source.reshape(2, 4, 3, 12, 256).transpose(0, 2, 1, 3, 4).reshape(6, 48, 256)
    u = gauge_field.reshape(4, 2, 3, 3, 256).transpose(0, 2, 3, 1, 4).reshape(72, 256).astype(F32)
    pairs = routes(nt, nz)

    def exchange(edges):
        return [lax.ppermute(e, ("ta", "gz"), p) for e, p in zip(edges, pairs)]

    edges = call(first_edges, "first_edges", [HALF] * 4, flags, field, u)
    halo = exchange(edges)
    acc = call(space_hops, "space_hops", SUM, None, field, u)
    field, *edges = call(finish_and_edges, "finish_and_edges", [SPINOR] + [HALF] * 4, flags, field, u, acc, *halo)
    halo = exchange(edges)
    acc = call(space_hops, "space_hops", SUM, None, field, u)
    field = call(finish, "finish", SPINOR, flags, field, u, acc, *halo)
    return field.reshape(2, 3, 4, 12, 256).transpose(0, 2, 1, 3, 4).reshape(source.shape)


def solution(mesh):
    spec = P("ta", "gz", None, None, None, None, None)
    return jax.shard_map(body, mesh=mesh, in_specs=(spec, spec), out_specs=spec, check_vma=False)
```

profile of v0, /device:TPU:1, one launch (start us, length us, event | category | flops | bytes accessed | tf_op | source)
XLA Modules:
  0.0 56.6 jit_solution(10582129851170796454)
XLA Ops:
  0.0 0.0 copy-start.1
  0.0 0.0 copy-start
  0.0 0.8 %copy-done.1 = bf16[1,1,4,2,3,3,256]{6,3,5,4,2,1,0:T(2,128)(2,1)S(1)} copy-done((bf16[1,1,4,2,3,3,256]{6,3,5,4,2,1,0:T(2,128)(2,1)S(1)}, bf16[1,1,4,2,3,3,256]{6,3,5,4,2,1,0:T(2,128)(2,1)}, u32[]{:S(2)}) %copy-start.1) | copy-done | bytes 36888
  0.8 0.1 reshape.22.u_ref
  0.9 0.1 copy-done
  1.0 0.6 %pad_maximum_fusion.flag_ref = f32[3]{0:T(128)} fusion(f32[1]{0:T(128)} %bitcast.2, f32[1]{0:T(128)} %bitcast.1, f32[1]{0:T(128)} %bitcast), kind=kLoop, calls=%fused_computation.1 | loop fusion | flops 6 | bytes 24 | tf_op jit(solution)/shard_map/stack | solution.py:256
  1.6 0.9 %first_edges.1 = (bf16[6,24,256]{2,1,0:T(8,128)(2,1)S(1)}, bf16[6,24,256]{2,1,0:T(8,128)(2,1)S(1)}, bf16[6,24,256]{2,1,0:T(8,128)(2,1)S(1)}, bf16[6,24,256]{2,1,0:T(8,128)(2,1)S(1)}) custom-call(f32[3]{0:T(128)} %pad_maximum_fusion.flag_ref, bf16[6,48,256]{2,1,0:T(8,128)(2,1)S(1)} %reshape.19.f_ref, f32[72,256]{1,0:T(8,128)S(1)} %reshape.22.u_ref), custom_call_target="tpu_custom_call" | custom-call | tf_op jit(solution)/shard_map/first_edges/pallas_call | solution.py:229
  2.5 17.3 %collective-permute-start = (bf16[6,24,256]{2,1,0:T(8,128)(2,1)S(1)}, bf16[6,24,256]{2,1,0:T(8,128)(2,1)S(1)}, u32[]{:S(2)}, u32[]{:S(2)}) collective-permute-start(bf16[6,24,256]{2,1,0:T(8,128)(2,1)S(1)} %get-tuple-element.14), channel_id=1, source_target_pairs={{0,1},{1,2},{2,3},{3,4},{4,5},{5,6},{6,7},{7,8},{8,9},{9,10},{10,1... | collective-permute-start | bytes 221192 | tf_op jit(solution)/shard_map/ppermute | solution.py:268
  19.8 1.9 %collective-permute-start.1 = (bf16[6,24,256]{2,1,0:T(8,128)(2,1)S(1)}, bf16[6,24,256]{2,1,0:T(8,128)(2,1)S(1)}, u32[]{:S(2)}, u32[]{:S(2)}) collective-permute-start(bf16[6,24,256]{2,1,0:T(8,128)(2,1)S(1)} %get-tuple-element.15), channel_id=1, source_target_pairs={{0,15},{1,0},{2,1},{3,2},{4,3},{5,4},{6,5},{7,6},{8,7},{9,8},{10,9... | collective-permute-start | bytes 221192 | tf_op jit(solution)/shard_map/ppermute | solution.py:268
  21.7 4.1 %collective-permute-start.2 = (bf16[6,24,256]{2,1,0:T(8,128)(2,1)S(1)}, bf16[6,24,256]{2,1,0:T(8,128)(2,1)S(1)}, u32[]{:S(2)}, u32[]{:S(2)}) collective-permute-start(bf16[6,24,256]{2,1,0:T(8,128)(2,1)S(1)} %get-tuple-element.16), channel_id=1, source_target_pairs={{0,16},{1,17},{2,18},{3,19},{4,20},{5,21},{6,22},{7,23},{8,24},{9,... | collective-permute-start | bytes 221192 | tf_op jit(solution)/shard_map/ppermute | solution.py:268
  25.8 1.9 %collective-permute-start.3 = (bf16[6,24,256]{2,1,0:T(8,128)(2,1)S(1)}, bf16[6,24,256]{2,1,0:T(8,128)(2,1)S(1)}, u32[]{:S(2)}, u32[]{:S(2)}) collective-permute-start(bf16[6,24,256]{2,1,0:T(8,128)(2,1)S(1)} %get-tuple-element.17), channel_id=1, source_target_pairs={{0,752},{1,753},{2,754},{3,755},{4,756},{5,757},{6,758},{7,759},{8... | collective-permute-start | bytes 221192 | tf_op jit(solution)/shard_map/ppermute | solution.py:268
  27.8 0.4 space_hops.2.acc_ref
  28.2 0.0 collective-permute-done.z1
  28.2 2.4 %collective-permute-done.1.z2 = bf16[6,24,256]{2,1,0:T(8,128)(2,1)S(1)} collective-permute-done((bf16[6,24,256]{2,1,0:T(8,128)(2,1)S(1)}, bf16[6,24,256]{2,1,0:T(8,128)(2,1)S(1)}, u32[]{:S(2)}, u32[]{:S(2)}) %collective-permute-start.1) | collective-permute-done | bytes 73760 | tf_op jit(solution)/shard_map/ppermute | solution.py:268
  30.6 0.0 collective-permute-done.2.t1
  30.6 1.7 %collective-permute-done.3.t2 = bf16[6,24,256]{2,1,0:T(8,128)(2,1)S(1)} collective-permute-done((bf16[6,24,256]{2,1,0:T(8,128)(2,1)S(1)}, bf16[6,24,256]{2,1,0:T(8,128)(2,1)S(1)}, u32[]{:S(2)}, u32[]{:S(2)}) %collective-permute-start.3) | collective-permute-done | bytes 73760 | tf_op jit(solution)/shard_map/ppermute | solution.py:268
  32.3 1.1 %finish_and_edges.1 = (bf16[6,48,256]{2,1,0:T(8,128)(2,1)S(1)}, bf16[6,24,256]{2,1,0:T(8,128)(2,1)S(1)}, bf16[6,24,256]{2,1,0:T(8,128)(2,1)S(1)}, bf16[6,24,256]{2,1,0:T(8,128)(2,1)S(1)}, bf16[6,24,256]{2,1,0:T(8,128)(2,1)S(1)}) custom-call(f32[3]{0:T(128)} %pad_maximum_fusion.flag_ref, bf16[6,48,256]{2,1,0:T(8,128)(2,1)S(1)} %reshape.19.f_ref, ...), custom_call_target="tpu_custom_call" | custom-call | tf_op jit(solution)/shard_map/finish_and_edges/pallas_call | solution.py:229
  33.4 5.5 %collective-permute-start.4 = (bf16[6,24,256]{2,1,0:T(8,128)(2,1)S(1)}, bf16[6,24,256]{2,1,0:T(8,128)(2,1)S(1)}, u32[]{:S(2)}, u32[]{:S(2)}) collective-permute-start(bf16[6,24,256]{2,1,0:T(8,128)(2,1)S(1)} %get-tuple-element.19), channel_id=1, source_target_pairs={{0,1},{1,2},{2,3},{3,4},{4,5},{5,6},{6,7},{7,8},{8,9},{9,10},{10,1... | collective-permute-start | bytes 221192 | tf_op jit(solution)/shard_map/ppermute | solution.py:268
  38.9 1.9 %collective-permute-start.5 = (bf16[6,24,256]{2,1,0:T(8,128)(2,1)S(1)}, bf16[6,24,256]{2,1,0:T(8,128)(2,1)S(1)}, u32[]{:S(2)}, u32[]{:S(2)}) collective-permute-start(bf16[6,24,256]{2,1,0:T(8,128)(2,1)S(1)} %get-tuple-element.20), channel_id=1, source_target_pairs={{0,15},{1,0},{2,1},{3,2},{4,3},{5,4},{6,5},{7,6},{8,7},{9,8},{10,9... | collective-permute-start | bytes 221192 | tf_op jit(solution)/shard_map/ppermute | solution.py:268
  40.9 8.3 %collective-permute-start.6 = (bf16[6,24,256]{2,1,0:T(8,128)(2,1)S(1)}, bf16[6,24,256]{2,1,0:T(8,128)(2,1)S(1)}, u32[]{:S(2)}, u32[]{:S(2)}) collective-permute-start(bf16[6,24,256]{2,1,0:T(8,128)(2,1)S(1)} %get-tuple-element.21), channel_id=1, source_target_pairs={{0,16},{1,17},{2,18},{3,19},{4,20},{5,21},{6,22},{7,23},{8,24},{9,... | collective-permute-start | bytes 221192 | tf_op jit(solution)/shard_map/ppermute | solution.py:268
  49.1 1.9 %collective-permute-start.7 = (bf16[6,24,256]{2,1,0:T(8,128)(2,1)S(1)}, bf16[6,24,256]{2,1,0:T(8,128)(2,1)S(1)}, u32[]{:S(2)}, u32[]{:S(2)}) collective-permute-start(bf16[6,24,256]{2,1,0:T(8,128)(2,1)S(1)} %get-tuple-element.22), channel_id=1, source_target_pairs={{0,752},{1,753},{2,754},{3,755},{4,756},{5,757},{6,758},{7,759},{8... | collective-permute-start | bytes 221192 | tf_op jit(solution)/shard_map/ppermute | solution.py:268
  51.1 0.4 space_hops.3.acc_ref
  51.5 0.0 collective-permute-done.4.z_one
  51.5 0.0 collective-permute-done.5.z_two
  51.5 0.0 collective-permute-done.6.t_near
  51.5 3.3 %collective-permute-done.7.t_far = bf16[6,24,256]{2,1,0:T(8,128)(2,1)S(1)} collective-permute-done((bf16[6,24,256]{2,1,0:T(8,128)(2,1)S(1)}, bf16[6,24,256]{2,1,0:T(8,128)(2,1)S(1)}, u32[]{:S(2)}, u32[]{:S(2)}) %collective-permute-start.7) | collective-permute-done | bytes 73760 | tf_op jit(solution)/shard_map/ppermute | solution.py:268
  54.8 1.0 %finish.1 = bf16[6,48,256]{2,1,0:T(8,128)(2,1)S(1)} custom-call(f32[3]{0:T(128)} %pad_maximum_fusion.flag_ref, bf16[6,48,256]{2,1,0:T(8,128)(2,1)S(1)} %get-tuple-element.18.f_ref, f32[72,256]{1,0:T(8,128)S(1)} %reshape.22.u_ref, f32[6,48,256]{2,1,0:T(8,128)S(1)} %space_hops.3.acc_ref, bf16[6,24,256]{2,1,0:T(8,128)(2,1)S(1)} %collective-permute-done.4.z_one, ...), custom_call_target="tpu_custom_call" | custom-call | tf_op jit(solution)/shard_map/finish/pallas_call | solution.py:229
  55.8 0.7 %copy.6 = bf16[1,1,2,4,3,12,256]{6,3,5,4,2,1,0:T(4,128)(2,1)} copy(bf16[1,1,2,4,3,12,256]{6,5,3,4,2,1,0:T(8,128)(2,1)S(1)} %bitcast.14) | data formatting | bytes 294912 | tf_op jit(solution)/shard_map/reshape | solution.py:277
  (4 shorter events, 0.1 us)
Async XLA Ops:
  0.0 0.8 %copy-start.1 = (bf16[1,1,4,2,3,3,256]{6,3,5,4,2,1,0:T(2,128)(2,1)S(1)}, bf16[1,1,4,2,3,3,256]{6,3,5,4,2,1,0:T(2,128)(2,1)}, u32[]{:S(2)}) copy-start(bf16[1,1,4,2,3,3,256]{6,3,5,4,2,1,0:T(2,128)(2,1)} %param.3) | copy-start | bytes 110596
  0.0 0.9 %copy-start = (bf16[1,1,2,4,3,12,256]{6,3,5,4,2,1,0:T(4,128)(2,1)S(1)}, bf16[1,1,2,4,3,12,256]{6,3,5,4,2,1,0:T(4,128)(2,1)}, u32[]{:S(2)}) copy-start(bf16[1,1,2,4,3,12,256]{6,3,5,4,2,1,0:T(4,128)(2,1)} %param.2) | copy-start | bytes 442372
  2.5 25.7 %collective-permute-start = (bf16[6,24,256]{2,1,0:T(8,128)(2,1)S(1)}, bf16[6,24,256]{2,1,0:T(8,128)(2,1)S(1)}, u32[]{:S(2)}, u32[]{:S(2)}) collective-permute-start(bf16[6,24,256]{2,1,0:T(8,128)(2,1)S(1)} %get-tuple-element.14), channel_id=1, source_target_pairs={{0,1},{1,2},{2,3},{3,4},{4,5},{5,6},{6,7},{7,8},{8,9},{9,10},{10,1... | collective-permute-start | bytes 221192 | tf_op jit(solution)/shard_map/ppermute | solution.py:268
  19.8 10.8 %collective-permute-start.1 = (bf16[6,24,256]{2,1,0:T(8,128)(2,1)S(1)}, bf16[6,24,256]{2,1,0:T(8,128)(2,1)S(1)}, u32[]{:S(2)}, u32[]{:S(2)}) collective-permute-start(bf16[6,24,256]{2,1,0:T(8,128)(2,1)S(1)} %get-tuple-element.15), channel_id=1, source_target_pairs={{0,15},{1,0},{2,1},{3,2},{4,3},{5,4},{6,5},{7,6},{8,7},{9,8},{10,9... | collective-permute-start | bytes 221192 | tf_op jit(solution)/shard_map/ppermute | solution.py:268
  21.7 8.9 %collective-permute-start.2 = (bf16[6,24,256]{2,1,0:T(8,128)(2,1)S(1)}, bf16[6,24,256]{2,1,0:T(8,128)(2,1)S(1)}, u32[]{:S(2)}, u32[]{:S(2)}) collective-permute-start(bf16[6,24,256]{2,1,0:T(8,128)(2,1)S(1)} %get-tuple-element.16), channel_id=1, source_target_pairs={{0,16},{1,17},{2,18},{3,19},{4,20},{5,21},{6,22},{7,23},{8,24},{9,... | collective-permute-start | bytes 221192 | tf_op jit(solution)/shard_map/ppermute | solution.py:268
  25.8 6.4 %collective-permute-start.3 = (bf16[6,24,256]{2,1,0:T(8,128)(2,1)S(1)}, bf16[6,24,256]{2,1,0:T(8,128)(2,1)S(1)}, u32[]{:S(2)}, u32[]{:S(2)}) collective-permute-start(bf16[6,24,256]{2,1,0:T(8,128)(2,1)S(1)} %get-tuple-element.17), channel_id=1, source_target_pairs={{0,752},{1,753},{2,754},{3,755},{4,756},{5,757},{6,758},{7,759},{8... | collective-permute-start | bytes 221192 | tf_op jit(solution)/shard_map/ppermute | solution.py:268
  33.4 18.0 %collective-permute-start.4 = (bf16[6,24,256]{2,1,0:T(8,128)(2,1)S(1)}, bf16[6,24,256]{2,1,0:T(8,128)(2,1)S(1)}, u32[]{:S(2)}, u32[]{:S(2)}) collective-permute-start(bf16[6,24,256]{2,1,0:T(8,128)(2,1)S(1)} %get-tuple-element.19), channel_id=1, source_target_pairs={{0,1},{1,2},{2,3},{3,4},{4,5},{5,6},{6,7},{7,8},{8,9},{9,10},{10,1... | collective-permute-start | bytes 221192 | tf_op jit(solution)/shard_map/ppermute | solution.py:268
  38.9 12.5 %collective-permute-start.5 = (bf16[6,24,256]{2,1,0:T(8,128)(2,1)S(1)}, bf16[6,24,256]{2,1,0:T(8,128)(2,1)S(1)}, u32[]{:S(2)}, u32[]{:S(2)}) collective-permute-start(bf16[6,24,256]{2,1,0:T(8,128)(2,1)S(1)} %get-tuple-element.20), channel_id=1, source_target_pairs={{0,15},{1,0},{2,1},{3,2},{4,3},{5,4},{6,5},{7,6},{8,7},{9,8},{10,9... | collective-permute-start | bytes 221192 | tf_op jit(solution)/shard_map/ppermute | solution.py:268
  40.9 10.6 %collective-permute-start.6 = (bf16[6,24,256]{2,1,0:T(8,128)(2,1)S(1)}, bf16[6,24,256]{2,1,0:T(8,128)(2,1)S(1)}, u32[]{:S(2)}, u32[]{:S(2)}) collective-permute-start(bf16[6,24,256]{2,1,0:T(8,128)(2,1)S(1)} %get-tuple-element.21), channel_id=1, source_target_pairs={{0,16},{1,17},{2,18},{3,19},{4,20},{5,21},{6,22},{7,23},{8,24},{9,... | collective-permute-start | bytes 221192 | tf_op jit(solution)/shard_map/ppermute | solution.py:268
  49.1 5.7 %collective-permute-start.7 = (bf16[6,24,256]{2,1,0:T(8,128)(2,1)S(1)}, bf16[6,24,256]{2,1,0:T(8,128)(2,1)S(1)}, u32[]{:S(2)}, u32[]{:S(2)}) collective-permute-start(bf16[6,24,256]{2,1,0:T(8,128)(2,1)S(1)} %get-tuple-element.22), channel_id=1, source_target_pairs={{0,752},{1,753},{2,754},{3,755},{4,756},{5,757},{6,758},{7,759},{8... | collective-permute-start | bytes 221192 | tf_op jit(solution)/shard_map/ppermute | solution.py:268
where the time goes:
time: 56.9 us; the launch traced here: 56.6 us
  starting transfers between devices  42.9 us (75%)
  waiting for transfers between devices  7.42 us (13%)
  Pallas kernels  3.78 us (7%)
  local copies, waits for them, and re-layouts  1.73 us (3%)
  other arithmetic  0.62 us (1%)
    ppermute x8, starting transfers between devices, exchange(): return [lax.ppermute(e, ('ta', 'gz'), p) for e, p in zip(edges, pairs)]  42.9 us
    ppermute x8, waiting for transfers between devices, exchange(): return [lax.ppermute(e, ('ta', 'gz'), p) for e, p in zip(edges, pairs)]  7.42 us
    pallas_call x5, Pallas kernels, call(): pl.pallas_call(kernel, out_shape=outs, in_specs=specs, out_specs=[in_vmem...  3.78 us
  transfers between devices with their start and end apart: 8, of which 3 were waited for; matrix products, arithmetic and copies ran while one was open for 0% of the time, Pallas kernels for 1%

commit v1 on v0

--- a/solution.py
+++ b/solution.py
@@ -114,8 +114,11 @@
     return [jnp.where(inside, a, b), jnp.where(inside, b, a)]
 
 
-def project_edges(field, u_ref, flag_ref, z_one, z_two, t_near, t_far):
-    odd = flag_ref[0] > 0.5
+def project_edges(field, u_ref, z_one, z_two, t_far, t_near):
+    ta = lax.axis_index("ta")
+    turn_back = jnp.where(ta == 0, -1.0, 1.0).astype(F32)
+    turn_on = jnp.where(ta == lax.axis_size("ta") - 1, -1.0, 1.0).astype(F32)
+    odd = lax.axis_index("ta") % 2 == 1
     for j in range(2):
         for mu, first, second in ((2, z_one, z_two), (3, t_near, t_far)):
             u = links(u_ref, mu, j)
@@ -125,16 +128,16 @@
                 fwd = mix(mu, r, up, dn, 1)
                 bwd = times(u, mix(mu, r, up, dn, -1), True)
                 if mu == 3:
-                    fwd = [v * flag_ref[1] for v in fwd]
-                    bwd = [v * flag_ref[2] for v in bwd]
+                    fwd = [v * turn_back for v in fwd]
+                    bwd = [v * turn_on for v in bwd]
                 for k in range(6):
                     at = (k, slice(r * 8, r * 8 + 8), slice(j * LANES, (j + 1) * LANES))
                     first[at] = jnp.where(odd, fwd[k], bwd[k]).astype(BF16)
                     second[at] = jnp.where(odd, bwd[k], fwd[k]).astype(BF16)
 
 
-def first_edges(flag_ref, f_ref, u_ref, z_one, z_two, t_near, t_far):
-    project_edges(lambda k, r, j: get(f_ref, k, r, j), u_ref, flag_ref, z_one, z_two, t_near, t_far)
+def first_edges(f_ref, u_ref, z_one, z_two, t_far, t_near):
+    project_edges(lambda k, r, j: get(f_ref, k, r, j), u_ref, z_one, z_two, t_far, t_near)
 
 
 def space_hops(f_ref, u_ref, acc_ref):
@@ -178,8 +181,8 @@
                 acc_ref[k, 24 + r * 8 : 32 + r * 8, lanes] = dn_acc.pop((k, r, j))
 
 
-def finish(flag_ref, f_ref, u_ref, acc_ref, z_one, z_two, t_near, t_far, out_ref):
-    odd = flag_ref[0] > 0.5
+def finish(f_ref, u_ref, acc_ref, z_one, z_two, t_far, t_near, out_ref):
+    odd = lax.axis_index("ta") % 2 == 1
     for j in range(2):
         lanes = slice(j * LANES, (j + 1) * LANES)
         uz = links(u_ref, 2, j)
@@ -208,9 +211,9 @@
                     out_ref[k, at * 8 : at * 8 + 8, lanes] = value.astype(BF16)
 
 
-def finish_and_edges(flag_ref, f_ref, u_ref, acc_ref, z1, z2, t1, t2, out_ref, z_one, z_two, t_near, t_far):
-    finish(flag_ref, f_ref, u_ref, acc_ref, z1, z2, t1, t2, out_ref)
-    project_edges(lambda k, r, j: get(out_ref, k, r, j), u_ref, flag_ref, z_one, z_two, t_near, t_far)
+def finish_and_edges(f_ref, u_ref, acc_ref, z1, z2, t1, t2, out_ref, z_one, z_two, t_far, t_near):
+    finish(f_ref, u_ref, acc_ref, z1, z2, t1, t2, out_ref)
+    project_edges(lambda k, r, j: get(out_ref, k, r, j), u_ref, z_one, z_two, t_far, t_near)
 
 
 SPINOR = pltpu.VMEM((6, 48, 256), BF16)
@@ -218,25 +221,20 @@
 SUM = pltpu.VMEM((6, 48, 256), F32)
 
 
-def call(kernel, name, outs, flags, *args):
+def call(kernel, name, outs, *args):
     in_vmem = pl.BlockSpec(memory_space=pltpu.VMEM)
-    specs = [in_vmem] * len(args)
-    args = tuple(pltpu.with_memory_space_constraint(a, pltpu.VMEM) for a in args)
-    given = args
-    if flags is not None:
-        specs = [pl.BlockSpec(memory_space=pltpu.SMEM)] + specs
-        given = (flags,) + args
+    args = [pltpu.with_memory_space_constraint(a, pltpu.VMEM) for a in args]
     return pl.pallas_call(
         kernel,
         out_shape=outs,
-        in_specs=specs,
+        in_specs=[in_vmem] * len(args),
         out_specs=[in_vmem] * len(outs) if isinstance(outs, list) else in_vmem,
         name=name,
-    )(*given)
+    )(*args)
 
 
 def routes(nt, nz):
-    z_one, z_two, t_near, t_far = [], [], [], []
+    z_one, z_two, t_far, t_near = [], [], [], []
     for t in range(nt):
         for z in range(nz):
             here = t * nz + z
@@ -247,19 +245,11 @@
             z_two.append((here, ahead if odd else behind))
             t_near.append((here, earlier if odd else later))
             t_far.append((here, later if odd else earlier))
-    return z_one, z_two, t_near, t_far
+    return z_one, z_two, t_far, t_near
 
 
 def body(source, gauge_field):
     nt, nz = lax.axis_size("ta"), lax.axis_size("gz")
-    ta = lax.axis_index("ta")
-    flags = jnp.stack(
-        [
-            (ta % 2).astype(F32),
-            jnp.where(ta == 0, -1.0, 1.0).astype(F32),
-            jnp.where(ta == nt - 1, -1.0, 1.0).astype(F32),
-        ]
-    )
     field = source.reshape(2, 4, 3, 12, 256).transpose(0, 2, 1, 3, 4).reshape(6, 48, 256)
     u = gauge_field.reshape(4, 2, 3, 3, 256).transpose(0, 2, 3, 1, 4).reshape(72, 256).astype(F32)
     pairs = routes(nt, nz)
@@ -267,13 +257,13 @@
     def exchange(edges):
         return [lax.ppermute(e, ("ta", "gz"), p) for e, p in zip(edges, pairs)]
 
-    edges = call(first_edges, "first_edges", [HALF] * 4, flags, field, u)
+    edges = call(first_edges, "first_edges", [HALF] * 4, field, u)
     halo = exchange(edges)
-    acc = call(space_hops, "space_hops", SUM, None, field, u)
-    field, *edges = call(finish_and_edges, "finish_and_edges", [SPINOR] + [HALF] * 4, flags, field, u, acc, *halo)
+    acc = call(space_hops, "space_hops", SUM, field, u)
+    field, *edges = call(finish_and_edges, "finish_and_edges", [SPINOR] + [HALF] * 4, field, u, acc, *halo)
     halo = exchange(edges)
-    acc = call(space_hops, "space_hops", SUM, None, field, u)
-    field = call(finish, "finish", SPINOR, flags, field, u, acc, *halo)
+    acc = call(space_hops, "space_hops", SUM, field, u)
+    field = call(finish, "finish", SPINOR, field, u, acc, *halo)
     return field.reshape(2, 3, 4, 12, 256).transpose(0, 2, 1, 3, 4).reshape(source.shape)
 
 

time: 56.9 us -> 51.6 us (0.907)
  waiting for transfers between devices: 7.42 us -> 0.94 us
  starting transfers between devices: 42.9 us -> 46.6 us
  Pallas kernels: 3.78 us -> 1.82 us
  local copies, waits for them, and re-layouts: 1.73 us -> 0.92 us
    ppermute x8, waiting for transfers between devices: 7.42 us -> 0.94 us  [exchange(): return [lax.ppermute(e, ('ta', 'gz'), p) for e, p in zip(edges, pairs)]]
    ppermute x8, starting transfers between devices: 42.9 us -> 46.6 us  [exchange(): return [lax.ppermute(e, ('ta', 'gz'), p) for e, p in zip(edges, pairs)]]
    pallas_call x5, Pallas kernels: 3.78 us -> 1.82 us  [call(): pl.pallas_call(kernel, out_shape=outs, in_specs=[in_vmem] * len(args), ou...]
    unnamed x4 -> x2, local copies, waits for them, and re-layouts: 0.84 us -> 0.03 us
    convert_element_type x1, other arithmetic: 0.03 us -> 0.83 us  [body(): gauge_field.reshape(4, 2, 3, 3, 256).transpose(0, 2, 3, 1, 4)]
    another operation x1 -> x0, other arithmetic: 0.6 us -> none  [body(): jnp.stack([(ta % 2).astype(F32), jnp.where(ta == 0, -1.0, 1.0).astype(F32...]
  transfers between devices with their start and end apart: 8 -> 8, of which waited for: 3 -> 3; matrix products, arithmetic and copies ran while one was open for 0% -> 0% of each run, Pallas kernels for 1% -> 2%
where the time goes in v1:
time: 51.6 us; the launch traced here: 51.3 us
  starting transfers between devices  46.6 us (90%)
  Pallas kernels  1.82 us (4%)
  waiting for transfers between devices  0.94 us (2%)
  local copies, waits for them, and re-layouts  0.92 us (2%)
  other arithmetic  0.83 us (2%)
    ppermute x8, starting transfers between devices, exchange(): return [lax.ppermute(e, ('ta', 'gz'), p) for e, p in zip(edges, pairs)]  46.6 us
    pallas_call x5, Pallas kernels, call(): pl.pallas_call(kernel, out_shape=outs, in_specs=[in_vmem] * len(args), ou...  1.82 us
  transfers between devices with their start and end apart: 8, of which 3 were waited for; matrix products, arithmetic and copies ran while one was open for 0% of the time, Pallas kernels for 2%

profile of v1, /device:TPU:1, one launch (start us, length us, event | category | flops | bytes accessed | tf_op | source)
XLA Modules:
  0.0 51.3 jit_solution(10456425400981178771)
XLA Ops:
  0.0 0.0 copy-start
  0.0 0.8 %convert_bitcast_fusion = f32[4,3,3,2,256]{4,3,2,1,0:T(2,128)S(1)} fusion(bf16[1,1,4,2,3,3,256]{6,3,5,4,2,1,0:T(2,128)(2,1)} %param.3), kind=kLoop, calls=%fused_computation | loop fusion | flops 18432 | bytes 110592 | tf_op jit(solution)/shard_map/convert_element_type | solution.py:254
  0.8 0.1 reshape.22.u_ref
  0.9 0.0 copy-done
  1.0 0.2 first_edges.1
  1.2 17.3 %collective-permute-start = (bf16[6,24,256]{2,1,0:T(8,128)(2,1)S(1)}, bf16[6,24,256]{2,1,0:T(8,128)(2,1)S(1)}, u32[]{:S(2)}, u32[]{:S(2)}) collective-permute-start(bf16[6,24,256]{2,1,0:T(8,128)(2,1)S(1)} %get-tuple-element.14), channel_id=1, source_target_pairs={{0,1},{1,2},{2,3},{3,4},{4,5},{5,6},{6,7},{7,8},{8,9},{9,10},{10,1... | collective-permute-start | bytes 221192 | tf_op jit(solution)/shard_map/ppermute | solution.py:258
  18.5 1.9 %collective-permute-start.1 = (bf16[6,24,256]{2,1,0:T(8,128)(2,1)S(1)}, bf16[6,24,256]{2,1,0:T(8,128)(2,1)S(1)}, u32[]{:S(2)}, u32[]{:S(2)}) collective-permute-start(bf16[6,24,256]{2,1,0:T(8,128)(2,1)S(1)} %get-tuple-element.15), channel_id=1, source_target_pairs={{0,15},{1,0},{2,1},{3,2},{4,3},{5,4},{6,5},{7,6},{8,7},{9,8},{10,9... | collective-permute-start | bytes 221192 | tf_op jit(solution)/shard_map/ppermute | solution.py:258
  20.4 3.9 %collective-permute-start.2 = (bf16[6,24,256]{2,1,0:T(8,128)(2,1)S(1)}, bf16[6,24,256]{2,1,0:T(8,128)(2,1)S(1)}, u32[]{:S(2)}, u32[]{:S(2)}) collective-permute-start(bf16[6,24,256]{2,1,0:T(8,128)(2,1)S(1)} %get-tuple-element.16), channel_id=1, source_target_pairs={{0,752},{1,753},{2,754},{3,755},{4,756},{5,757},{6,758},{7,759},{8... | collective-permute-start | bytes 221192 | tf_op jit(solution)/shard_map/ppermute | solution.py:258
  24.4 5.3 %collective-permute-start.3 = (bf16[6,24,256]{2,1,0:T(8,128)(2,1)S(1)}, bf16[6,24,256]{2,1,0:T(8,128)(2,1)S(1)}, u32[]{:S(2)}, u32[]{:S(2)}) collective-permute-start(bf16[6,24,256]{2,1,0:T(8,128)(2,1)S(1)} %get-tuple-element.17), channel_id=1, source_target_pairs={{0,16},{1,17},{2,18},{3,19},{4,20},{5,21},{6,22},{7,23},{8,24},{9,... | collective-permute-start | bytes 221192 | tf_op jit(solution)/shard_map/ppermute | solution.py:258
  29.7 0.4 space_hops.2.acc_ref
  30.1 0.0 collective-permute-done.z1
  30.1 0.0 collective-permute-done.1.z2
  30.1 0.0 collective-permute-done.2.t1
  30.1 0.5 collective-permute-done.3.t2
  30.6 0.5 finish_and_edges.1
  31.1 8.5 %collective-permute-start.4 = (bf16[6,24,256]{2,1,0:T(8,128)(2,1)S(1)}, bf16[6,24,256]{2,1,0:T(8,128)(2,1)S(1)}, u32[]{:S(2)}, u32[]{:S(2)}) collective-permute-start(bf16[6,24,256]{2,1,0:T(8,128)(2,1)S(1)} %get-tuple-element.19), channel_id=1, source_target_pairs={{0,1},{1,2},{2,3},{3,4},{4,5},{5,6},{6,7},{7,8},{8,9},{9,10},{10,1... | collective-permute-start | bytes 221192 | tf_op jit(solution)/shard_map/ppermute | solution.py:258
  39.6 1.9 %collective-permute-start.5 = (bf16[6,24,256]{2,1,0:T(8,128)(2,1)S(1)}, bf16[6,24,256]{2,1,0:T(8,128)(2,1)S(1)}, u32[]{:S(2)}, u32[]{:S(2)}) collective-permute-start(bf16[6,24,256]{2,1,0:T(8,128)(2,1)S(1)} %get-tuple-element.20), channel_id=1, source_target_pairs={{0,15},{1,0},{2,1},{3,2},{4,3},{5,4},{6,5},{7,6},{8,7},{9,8},{10,9... | collective-permute-start | bytes 221192 | tf_op jit(solution)/shard_map/ppermute | solution.py:258
  41.5 1.9 %collective-permute-start.6 = (bf16[6,24,256]{2,1,0:T(8,128)(2,1)S(1)}, bf16[6,24,256]{2,1,0:T(8,128)(2,1)S(1)}, u32[]{:S(2)}, u32[]{:S(2)}) collective-permute-start(bf16[6,24,256]{2,1,0:T(8,128)(2,1)S(1)} %get-tuple-element.21), channel_id=1, source_target_pairs={{0,752},{1,753},{2,754},{3,755},{4,756},{5,757},{6,758},{7,759},{8... | collective-permute-start | bytes 221192 | tf_op jit(solution)/shard_map/ppermute | solution.py:258
  43.4 5.9 %collective-permute-start.7 = (bf16[6,24,256]{2,1,0:T(8,128)(2,1)S(1)}, bf16[6,24,256]{2,1,0:T(8,128)(2,1)S(1)}, u32[]{:S(2)}, u32[]{:S(2)}) collective-permute-start(bf16[6,24,256]{2,1,0:T(8,128)(2,1)S(1)} %get-tuple-element.22), channel_id=1, source_target_pairs={{0,16},{1,17},{2,18},{3,19},{4,20},{5,21},{6,22},{7,23},{8,24},{9,... | collective-permute-start | bytes 221192 | tf_op jit(solution)/shard_map/ppermute | solution.py:258
  49.3 0.4 space_hops.3.acc_ref
  49.7 0.0 collective-permute-done.4.z_one
  49.7 0.1 collective-permute-done.5.z_two
  49.8 0.0 collective-permute-done.6.t_far
  49.8 0.4 collective-permute-done.7.t_near
  50.2 0.3 finish.1
  50.5 0.7 %copy.6 = bf16[1,1,2,4,3,12,256]{6,3,5,4,2,1,0:T(4,128)(2,1)} copy(bf16[1,1,2,4,3,12,256]{6,5,3,4,2,1,0:T(8,128)(2,1)S(1)} %bitcast.11) | data formatting | bytes 294912 | tf_op jit(solution)/shard_map/reshape | solution.py:267
  (3 shorter events, 0.1 us)
Async XLA Ops:
  0.0 0.9 %copy-start = (bf16[1,1,2,4,3,12,256]{6,3,5,4,2,1,0:T(4,128)(2,1)S(1)}, bf16[1,1,2,4,3,12,256]{6,3,5,4,2,1,0:T(4,128)(2,1)}, u32[]{:S(2)}) copy-start(bf16[1,1,2,4,3,12,256]{6,3,5,4,2,1,0:T(4,128)(2,1)} %param.2) | copy-start | bytes 442372
  1.2 28.9 %collective-permute-start = (bf16[6,24,256]{2,1,0:T(8,128)(2,1)S(1)}, bf16[6,24,256]{2,1,0:T(8,128)(2,1)S(1)}, u32[]{:S(2)}, u32[]{:S(2)}) collective-permute-start(bf16[6,24,256]{2,1,0:T(8,128)(2,1)S(1)} %get-tuple-element.14), channel_id=1, source_target_pairs={{0,1},{1,2},{2,3},{3,4},{4,5},{5,6},{6,7},{7,8},{8,9},{9,10},{10,1... | collective-permute-start | bytes 221192 | tf_op jit(solution)/shard_map/ppermute | solution.py:258
  18.5 11.6 %collective-permute-start.1 = (bf16[6,24,256]{2,1,0:T(8,128)(2,1)S(1)}, bf16[6,24,256]{2,1,0:T(8,128)(2,1)S(1)}, u32[]{:S(2)}, u32[]{:S(2)}) collective-permute-start(bf16[6,24,256]{2,1,0:T(8,128)(2,1)S(1)} %get-tuple-element.15), channel_id=1, source_target_pairs={{0,15},{1,0},{2,1},{3,2},{4,3},{5,4},{6,5},{7,6},{8,7},{9,8},{10,9... | collective-permute-start | bytes 221192 | tf_op jit(solution)/shard_map/ppermute | solution.py:258
  20.4 9.7 %collective-permute-start.2 = (bf16[6,24,256]{2,1,0:T(8,128)(2,1)S(1)}, bf16[6,24,256]{2,1,0:T(8,128)(2,1)S(1)}, u32[]{:S(2)}, u32[]{:S(2)}) collective-permute-start(bf16[6,24,256]{2,1,0:T(8,128)(2,1)S(1)} %get-tuple-element.16), channel_id=1, source_target_pairs={{0,752},{1,753},{2,754},{3,755},{4,756},{5,757},{6,758},{7,759},{8... | collective-permute-start | bytes 221192 | tf_op jit(solution)/shard_map/ppermute | solution.py:258
  24.4 6.2 %collective-permute-start.3 = (bf16[6,24,256]{2,1,0:T(8,128)(2,1)S(1)}, bf16[6,24,256]{2,1,0:T(8,128)(2,1)S(1)}, u32[]{:S(2)}, u32[]{:S(2)}) collective-permute-start(bf16[6,24,256]{2,1,0:T(8,128)(2,1)S(1)} %get-tuple-element.17), channel_id=1, source_target_pairs={{0,16},{1,17},{2,18},{3,19},{4,20},{5,21},{6,22},{7,23},{8,24},{9,... | collective-permute-start | bytes 221192 | tf_op jit(solution)/shard_map/ppermute | solution.py:258
  31.1 18.6 %collective-permute-start.4 = (bf16[6,24,256]{2,1,0:T(8,128)(2,1)S(1)}, bf16[6,24,256]{2,1,0:T(8,128)(2,1)S(1)}, u32[]{:S(2)}, u32[]{:S(2)}) collective-permute-start(bf16[6,24,256]{2,1,0:T(8,128)(2,1)S(1)} %get-tuple-element.19), channel_id=1, source_target_pairs={{0,1},{1,2},{2,3},{3,4},{4,5},{5,6},{6,7},{7,8},{8,9},{9,10},{10,1... | collective-permute-start | bytes 221192 | tf_op jit(solution)/shard_map/ppermute | solution.py:258
  39.6 10.2 %collective-permute-start.5 = (bf16[6,24,256]{2,1,0:T(8,128)(2,1)S(1)}, bf16[6,24,256]{2,1,0:T(8,128)(2,1)S(1)}, u32[]{:S(2)}, u32[]{:S(2)}) collective-permute-start(bf16[6,24,256]{2,1,0:T(8,128)(2,1)S(1)} %get-tuple-element.20), channel_id=1, source_target_pairs={{0,15},{1,0},{2,1},{3,2},{4,3},{5,4},{6,5},{7,6},{8,7},{9,8},{10,9... | collective-permute-start | bytes 221192 | tf_op jit(solution)/shard_map/ppermute | solution.py:258
  41.5 8.3 %collective-permute-start.6 = (bf16[6,24,256]{2,1,0:T(8,128)(2,1)S(1)}, bf16[6,24,256]{2,1,0:T(8,128)(2,1)S(1)}, u32[]{:S(2)}, u32[]{:S(2)}) collective-permute-start(bf16[6,24,256]{2,1,0:T(8,128)(2,1)S(1)} %get-tuple-element.21), channel_id=1, source_target_pairs={{0,752},{1,753},{2,754},{3,755},{4,756},{5,757},{6,758},{7,759},{8... | collective-permute-start | bytes 221192 | tf_op jit(solution)/shard_map/ppermute | solution.py:258
  43.4 6.8 %collective-permute-start.7 = (bf16[6,24,256]{2,1,0:T(8,128)(2,1)S(1)}, bf16[6,24,256]{2,1,0:T(8,128)(2,1)S(1)}, u32[]{:S(2)}, u32[]{:S(2)}) collective-permute-start(bf16[6,24,256]{2,1,0:T(8,128)(2,1)S(1)} %get-tuple-element.22), channel_id=1, source_target_pairs={{0,16},{1,17},{2,18},{3,19},{4,20},{5,21},{6,22},{7,23},{8,24},{9,... | collective-permute-start | bytes 221192 | tf_op jit(solution)/shard_map/ppermute | solution.py:258

commit v2 on v1

--- a/solution.py
+++ b/solution.py
@@ -114,13 +114,18 @@
     return [jnp.where(inside, a, b), jnp.where(inside, b, a)]
 
 
+def flips():
+    ta = lax.axis_index("ta")
+    return ta % 2 == 1, lax.axis_index("gz") % 2 == 1
+
+
 def project_edges(field, u_ref, z_one, z_two, t_far, t_near):
     ta = lax.axis_index("ta")
+    flip_t, flip_z = flips()
     turn_back = jnp.where(ta == 0, -1.0, 1.0).astype(F32)
     turn_on = jnp.where(ta == lax.axis_size("ta") - 1, -1.0, 1.0).astype(F32)
-    odd = lax.axis_index("ta") % 2 == 1
     for j in range(2):
-        for mu, first, second in ((2, z_one, z_two), (3, t_near, t_far)):
+        for mu, flip, first, second in ((2, flip_z, z_one, z_two), (3, flip_t, t_near, t_far)):
             u = links(u_ref, mu, j)
             for r in range(3):
                 up = [field(k, r, j) for k in range(6)]
@@ -132,12 +137,20 @@
                     bwd = [v * turn_on for v in bwd]
                 for k in range(6):
                     at = (k, slice(r * 8, r * 8 + 8), slice(j * LANES, (j + 1) * LANES))
-                    first[at] = jnp.where(odd, fwd[k], bwd[k]).astype(BF16)
-                    second[at] = jnp.where(odd, bwd[k], fwd[k]).astype(BF16)
-
-
-def first_edges(f_ref, u_ref, z_one, z_two, t_far, t_near):
-    project_edges(lambda k, r, j: get(f_ref, k, r, j), u_ref, z_one, z_two, t_far, t_near)
+                    first[at] = jnp.where(flip, fwd[k], bwd[k]).astype(BF16)
+                    second[at] = jnp.where(flip, bwd[k], fwd[k]).astype(BF16)
+
+
+FIRST_ROUND = (0, 1, 2, 3)
+SECOND_ROUND = (1, 0, 2, 3)
+
+
+def in_place(order, items):
+    return [items[order.index(i)] for i in range(4)]
+
+
+def first_edges(f_ref, u_ref, *edges):
+    project_edges(lambda k, r, j: get(f_ref, k, r, j), u_ref, *in_place(FIRST_ROUND, edges))
 
 
 def space_hops(f_ref, u_ref, acc_ref):
@@ -181,8 +194,8 @@
                 acc_ref[k, 24 + r * 8 : 32 + r * 8, lanes] = dn_acc.pop((k, r, j))
 
 
-def finish(f_ref, u_ref, acc_ref, z_one, z_two, t_far, t_near, out_ref):
-    odd = lax.axis_index("ta") % 2 == 1
+def add_halo(f_ref, u_ref, acc_ref, z_one, z_two, t_far, t_near, out_ref):
+    flip_t, flip_z = flips()
     for j in range(2):
         lanes = slice(j * LANES, (j + 1) * LANES)
         uz = links(u_ref, 2, j)
@@ -196,10 +209,10 @@
             near = [get(t_near, k, r, j) for k in range(6)]
             far = [get(t_far, k, r, j) for k in range(6)]
             parts = (
-                (2, times(uz, [jnp.where(odd, a, b) for a, b in zip(one, two)], False), 1),
-                (2, [jnp.where(odd, b, a) for a, b in zip(one, two)], -1),
-                (3, times(ut, [jnp.where(odd, b, a) for a, b in zip(near, far)], False), 1),
-                (3, [jnp.where(odd, a, b) for a, b in zip(near, far)], -1),
+                (2, times(uz, [jnp.where(flip_z, b, a) for a, b in zip(one, two)], False), 1),
+                (2, [jnp.where(flip_z, a, b) for a, b in zip(one, two)], -1),
+                (3, times(ut, [jnp.where(flip_t, b, a) for a, b in zip(near, far)], False), 1),
+                (3, [jnp.where(flip_t, a, b) for a, b in zip(near, far)], -1),
             )
             for mu, k6, q in parts:
                 lower = spread(mu, r, k6, q)
@@ -211,9 +224,13 @@
                     out_ref[k, at * 8 : at * 8 + 8, lanes] = value.astype(BF16)
 
 
-def finish_and_edges(f_ref, u_ref, acc_ref, z1, z2, t1, t2, out_ref, z_one, z_two, t_far, t_near):
-    finish(f_ref, u_ref, acc_ref, z1, z2, t1, t2, out_ref)
-    project_edges(lambda k, r, j: get(out_ref, k, r, j), u_ref, z_one, z_two, t_far, t_near)
+def finish_and_edges(f_ref, u_ref, acc_ref, h0, h1, h2, h3, out_ref, *edges):
+    add_halo(f_ref, u_ref, acc_ref, *in_place(FIRST_ROUND, (h0, h1, h2, h3)), out_ref)
+    project_edges(lambda k, r, j: get(out_ref, k, r, j), u_ref, *in_place(SECOND_ROUND, edges))
+
+
+def finish(f_ref, u_ref, acc_ref, h0, h1, h2, h3, out_ref):
+    add_halo(f_ref, u_ref, acc_ref, *in_place(SECOND_ROUND, (h0, h1, h2, h3)), out_ref)
 
 
 SPINOR = pltpu.VMEM((6, 48, 256), BF16)
@@ -240,11 +257,10 @@
             here = t * nz + z
             ahead, behind = t * nz + (z + 1) % nz, t * nz + (z - 1) % nz
             later, earlier = (t + 1) % nt * nz + z, (t - 1) % nt * nz + z
-            odd = t % 2
-            z_one.append((here, behind if odd else ahead))
-            z_two.append((here, ahead if odd else behind))
-            t_near.append((here, earlier if odd else later))
-            t_far.append((here, later if odd else earlier))
+            z_one.append((here, behind if z % 2 else ahead))
+            z_two.append((here, ahead if z % 2 else behind))
+            t_near.append((here, earlier if t % 2 else later))
+            t_far.append((here, later if t % 2 else earlier))
     return z_one, z_two, t_far, t_near
 
 
@@ -254,14 +270,14 @@
     u = gauge_field.reshape(4, 2, 3, 3, 256).transpose(0, 2, 3, 1, 4).reshape(72, 256).astype(F32)
     pairs = routes(nt, nz)
 
-    def exchange(edges):
-        return [lax.ppermute(e, ("ta", "gz"), p) for e, p in zip(edges, pairs)]
+    def exchange(edges, order):
+        return [lax.ppermute(e, ("ta", "gz"), pairs[i]) for i, e in zip(order, edges)]
 
     edges = call(first_edges, "first_edges", [HALF] * 4, field, u)
-    halo = exchange(edges)
+    halo = exchange(edges, FIRST_ROUND)
     acc = call(space_hops, "space_hops", SUM, field, u)
     field, *edges = call(finish_and_edges, "finish_and_edges", [SPINOR] + [HALF] * 4, field, u, acc, *halo)
-    halo = exchange(edges)
+    halo = exchange(edges, SECOND_ROUND)
     acc = call(space_hops, "space_hops", SUM, field, u)
     field = call(finish, "finish", SPINOR, field, u, acc, *halo)
     return field.reshape(2, 3, 4, 12, 256).transpose(0, 2, 1, 3, 4).reshape(source.shape)

time: 51.6 us -> 49.2 us (0.953)
  the two profiles are of different devices: /device:TPU:1 before, /device:TPU:6 now
where the time goes in v2:
time: 49.2 us; the launch traced here: 48.9 us
  starting transfers between devices  41.2 us (84%)
  waiting for transfers between devices  4.01 us (8%)
  Pallas kernels  1.81 us (4%)
  local copies, waits for them, and re-layouts  0.92 us (2%)
  other arithmetic  0.83 us (2%)
    ppermute x8, starting transfers between devices, exchange(): lax.ppermute(e, ('ta', 'gz'), pairs[i])  41.2 us
    ppermute x8, waiting for transfers between devices, exchange(): lax.ppermute(e, ('ta', 'gz'), pairs[i])  4.01 us
    pallas_call x5, Pallas kernels, call(): pl.pallas_call(kernel, out_shape=outs, in_specs=[in_vmem] * len(args), ou...  1.81 us
  transfers between devices with their start and end apart: 8, of which 2 were waited for; matrix products, arithmetic and copies ran while one was open for 0% of the time, Pallas kernels for 2%

profile of v2, /device:TPU:6, one launch (start us, length us, event | category | flops | bytes accessed | tf_op | source)
XLA Modules:
  0.0 48.9 jit_solution(14574144799927942648)
XLA Ops:
  0.0 0.0 copy-start
  0.0 0.8 %convert_bitcast_fusion = f32[4,3,3,2,256]{4,3,2,1,0:T(2,128)S(1)} fusion(bf16[1,1,4,2,3,3,256]{6,3,5,4,2,1,0:T(2,128)(2,1)} %param.3), kind=kLoop, calls=%fused_computation | loop fusion | flops 18432 | bytes 110592 | tf_op jit(solution)/shard_map/convert_element_type | solution.py:270
  0.8 0.1 reshape.22.u_ref
  0.9 0.0 copy-done
  1.0 0.2 first_edges.1
  1.2 7.9 %collective-permute-start = (bf16[6,24,256]{2,1,0:T(8,128)(2,1)S(1)}, bf16[6,24,256]{2,1,0:T(8,128)(2,1)S(1)}, u32[]{:S(2)}, u32[]{:S(2)}) collective-permute-start(bf16[6,24,256]{2,1,0:T(8,128)(2,1)S(1)} %get-tuple-element.14), channel_id=1, source_target_pairs={{0,1},{1,0},{2,3},{3,2},{4,5},{5,4},{6,7},{7,6},{8,9},{9,8},{10,11... | collective-permute-start | bytes 221192 | tf_op jit(solution)/shard_map/ppermute | solution.py:274
  9.1 10.0 %collective-permute-start.1 = (bf16[6,24,256]{2,1,0:T(8,128)(2,1)S(1)}, bf16[6,24,256]{2,1,0:T(8,128)(2,1)S(1)}, u32[]{:S(2)}, u32[]{:S(2)}) collective-permute-start(bf16[6,24,256]{2,1,0:T(8,128)(2,1)S(1)} %get-tuple-element.15), channel_id=1, source_target_pairs={{0,15},{1,2},{2,1},{3,4},{4,3},{5,6},{6,5},{7,8},{8,7},{9,10},{10,... | collective-permute-start | bytes 221192 | tf_op jit(solution)/shard_map/ppermute | solution.py:274
  19.1 5.5 %collective-permute-start.2 = (bf16[6,24,256]{2,1,0:T(8,128)(2,1)S(1)}, bf16[6,24,256]{2,1,0:T(8,128)(2,1)S(1)}, u32[]{:S(2)}, u32[]{:S(2)}) collective-permute-start(bf16[6,24,256]{2,1,0:T(8,128)(2,1)S(1)} %get-tuple-element.16), channel_id=1, source_target_pairs={{0,752},{1,753},{2,754},{3,755},{4,756},{5,757},{6,758},{7,759},{8... | collective-permute-start | bytes 221192 | tf_op jit(solution)/shard_map/ppermute | solution.py:274
  24.6 1.9 %collective-permute-start.3 = (bf16[6,24,256]{2,1,0:T(8,128)(2,1)S(1)}, bf16[6,24,256]{2,1,0:T(8,128)(2,1)S(1)}, u32[]{:S(2)}, u32[]{:S(2)}) collective-permute-start(bf16[6,24,256]{2,1,0:T(8,128)(2,1)S(1)} %get-tuple-element.17), channel_id=1, source_target_pairs={{0,16},{1,17},{2,18},{3,19},{4,20},{5,21},{6,22},{7,23},{8,24},{9,... | collective-permute-start | bytes 221192 | tf_op jit(solution)/shard_map/ppermute | solution.py:274
  26.5 0.4 space_hops.2.acc_ref
  26.9 0.0 collective-permute-done.h0
  26.9 0.0 collective-permute-done.1.h1
  26.9 0.9 %collective-permute-done.2.h2 = bf16[6,24,256]{2,1,0:T(8,128)(2,1)S(1)} collective-permute-done((bf16[6,24,256]{2,1,0:T(8,128)(2,1)S(1)}, bf16[6,24,256]{2,1,0:T(8,128)(2,1)S(1)}, u32[]{:S(2)}, u32[]{:S(2)}) %collective-permute-start.2) | collective-permute-done | bytes 73760 | tf_op jit(solution)/shard_map/ppermute | solution.py:274
  27.9 0.0 collective-permute-done.3.h3
  27.9 0.5 finish_and_edges.1
  28.4 4.3 %collective-permute-start.4 = (bf16[6,24,256]{2,1,0:T(8,128)(2,1)S(1)}, bf16[6,24,256]{2,1,0:T(8,128)(2,1)S(1)}, u32[]{:S(2)}, u32[]{:S(2)}) collective-permute-start(bf16[6,24,256]{2,1,0:T(8,128)(2,1)S(1)} %get-tuple-element.19), channel_id=1, source_target_pairs={{0,15},{1,2},{2,1},{3,4},{4,3},{5,6},{6,5},{7,8},{8,7},{9,10},{10,... | collective-permute-start | bytes 221192 | tf_op jit(solution)/shard_map/ppermute | solution.py:274
  32.7 4.1 %collective-permute-start.5 = (bf16[6,24,256]{2,1,0:T(8,128)(2,1)S(1)}, bf16[6,24,256]{2,1,0:T(8,128)(2,1)S(1)}, u32[]{:S(2)}, u32[]{:S(2)}) collective-permute-start(bf16[6,24,256]{2,1,0:T(8,128)(2,1)S(1)} %get-tuple-element.20), channel_id=1, source_target_pairs={{0,1},{1,0},{2,3},{3,2},{4,5},{5,4},{6,7},{7,6},{8,9},{9,8},{10,11... | collective-permute-start | bytes 221192 | tf_op jit(solution)/shard_map/ppermute | solution.py:274
  36.8 5.6 %collective-permute-start.6 = (bf16[6,24,256]{2,1,0:T(8,128)(2,1)S(1)}, bf16[6,24,256]{2,1,0:T(8,128)(2,1)S(1)}, u32[]{:S(2)}, u32[]{:S(2)}) collective-permute-start(bf16[6,24,256]{2,1,0:T(8,128)(2,1)S(1)} %get-tuple-element.21), channel_id=1, source_target_pairs={{0,752},{1,753},{2,754},{3,755},{4,756},{5,757},{6,758},{7,759},{8... | collective-permute-start | bytes 221192 | tf_op jit(solution)/shard_map/ppermute | solution.py:274
  42.4 1.9 %collective-permute-start.7 = (bf16[6,24,256]{2,1,0:T(8,128)(2,1)S(1)}, bf16[6,24,256]{2,1,0:T(8,128)(2,1)S(1)}, u32[]{:S(2)}, u32[]{:S(2)}) collective-permute-start(bf16[6,24,256]{2,1,0:T(8,128)(2,1)S(1)} %get-tuple-element.22), channel_id=1, source_target_pairs={{0,16},{1,17},{2,18},{3,19},{4,20},{5,21},{6,22},{7,23},{8,24},{9,... | collective-permute-start | bytes 221192 | tf_op jit(solution)/shard_map/ppermute | solution.py:274
  44.3 0.4 space_hops.3.acc_ref
  44.7 0.0 collective-permute-done.4.h0
  44.7 0.0 collective-permute-done.5.h1
  44.7 3.0 %collective-permute-done.6.h2 = bf16[6,24,256]{2,1,0:T(8,128)(2,1)S(1)} collective-permute-done((bf16[6,24,256]{2,1,0:T(8,128)(2,1)S(1)}, bf16[6,24,256]{2,1,0:T(8,128)(2,1)S(1)}, u32[]{:S(2)}, u32[]{:S(2)}) %collective-permute-start.6) | collective-permute-done | bytes 73760 | tf_op jit(solution)/shard_map/ppermute | solution.py:274
  47.8 0.0 collective-permute-done.7.h3
  47.8 0.3 finish.1
  48.1 0.7 %copy.6 = bf16[1,1,2,4,3,12,256]{6,3,5,4,2,1,0:T(4,128)(2,1)} copy(bf16[1,1,2,4,3,12,256]{6,5,3,4,2,1,0:T(8,128)(2,1)S(1)} %bitcast.11) | data formatting | bytes 294912 | tf_op jit(solution)/shard_map/reshape | solution.py:283
  (3 shorter events, 0.1 us)
Async XLA Ops:
  0.0 0.9 %copy-start = (bf16[1,1,2,4,3,12,256]{6,3,5,4,2,1,0:T(4,128)(2,1)S(1)}, bf16[1,1,2,4,3,12,256]{6,3,5,4,2,1,0:T(4,128)(2,1)}, u32[]{:S(2)}) copy-start(bf16[1,1,2,4,3,12,256]{6,3,5,4,2,1,0:T(4,128)(2,1)} %param.2) | copy-start | bytes 442372
  1.2 25.7 %collective-permute-start = (bf16[6,24,256]{2,1,0:T(8,128)(2,1)S(1)}, bf16[6,24,256]{2,1,0:T(8,128)(2,1)S(1)}, u32[]{:S(2)}, u32[]{:S(2)}) collective-permute-start(bf16[6,24,256]{2,1,0:T(8,128)(2,1)S(1)} %get-tuple-element.14), channel_id=1, source_target_pairs={{0,1},{1,0},{2,3},{3,2},{4,5},{5,4},{6,7},{7,6},{8,9},{9,8},{10,11... | collective-permute-start | bytes 221192 | tf_op jit(solution)/shard_map/ppermute | solution.py:274
  9.1 17.8 %collective-permute-start.1 = (bf16[6,24,256]{2,1,0:T(8,128)(2,1)S(1)}, bf16[6,24,256]{2,1,0:T(8,128)(2,1)S(1)}, u32[]{:S(2)}, u32[]{:S(2)}) collective-permute-start(bf16[6,24,256]{2,1,0:T(8,128)(2,1)S(1)} %get-tuple-element.15), channel_id=1, source_target_pairs={{0,15},{1,2},{2,1},{3,4},{4,3},{5,6},{6,5},{7,8},{8,7},{9,10},{10,... | collective-permute-start | bytes 221192 | tf_op jit(solution)/shard_map/ppermute | solution.py:274
  19.1 8.8 %collective-permute-start.2 = (bf16[6,24,256]{2,1,0:T(8,128)(2,1)S(1)}, bf16[6,24,256]{2,1,0:T(8,128)(2,1)S(1)}, u32[]{:S(2)}, u32[]{:S(2)}) collective-permute-start(bf16[6,24,256]{2,1,0:T(8,128)(2,1)S(1)} %get-tuple-element.16), channel_id=1, source_target_pairs={{0,752},{1,753},{2,754},{3,755},{4,756},{5,757},{6,758},{7,759},{8... | collective-permute-start | bytes 221192 | tf_op jit(solution)/shard_map/ppermute | solution.py:274
  24.6 3.3 %collective-permute-start.3 = (bf16[6,24,256]{2,1,0:T(8,128)(2,1)S(1)}, bf16[6,24,256]{2,1,0:T(8,128)(2,1)S(1)}, u32[]{:S(2)}, u32[]{:S(2)}) collective-permute-start(bf16[6,24,256]{2,1,0:T(8,128)(2,1)S(1)} %get-tuple-element.17), channel_id=1, source_target_pairs={{0,16},{1,17},{2,18},{3,19},{4,20},{5,21},{6,22},{7,23},{8,24},{9,... | collective-permute-start | bytes 221192 | tf_op jit(solution)/shard_map/ppermute | solution.py:274
  28.4 16.3 %collective-permute-start.4 = (bf16[6,24,256]{2,1,0:T(8,128)(2,1)S(1)}, bf16[6,24,256]{2,1,0:T(8,128)(2,1)S(1)}, u32[]{:S(2)}, u32[]{:S(2)}) collective-permute-start(bf16[6,24,256]{2,1,0:T(8,128)(2,1)S(1)} %get-tuple-element.19), channel_id=1, source_target_pairs={{0,15},{1,2},{2,1},{3,4},{4,3},{5,6},{6,5},{7,8},{8,7},{9,10},{10,... | collective-permute-start | bytes 221192 | tf_op jit(solution)/shard_map/ppermute | solution.py:274
  32.7 12.0 %collective-permute-start.5 = (bf16[6,24,256]{2,1,0:T(8,128)(2,1)S(1)}, bf16[6,24,256]{2,1,0:T(8,128)(2,1)S(1)}, u32[]{:S(2)}, u32[]{:S(2)}) collective-permute-start(bf16[6,24,256]{2,1,0:T(8,128)(2,1)S(1)} %get-tuple-element.20), channel_id=1, source_target_pairs={{0,1},{1,0},{2,3},{3,2},{4,5},{5,4},{6,7},{7,6},{8,9},{9,8},{10,11... | collective-permute-start | bytes 221192 | tf_op jit(solution)/shard_map/ppermute | solution.py:274
  36.8 11.0 %collective-permute-start.6 = (bf16[6,24,256]{2,1,0:T(8,128)(2,1)S(1)}, bf16[6,24,256]{2,1,0:T(8,128)(2,1)S(1)}, u32[]{:S(2)}, u32[]{:S(2)}) collective-permute-start(bf16[6,24,256]{2,1,0:T(8,128)(2,1)S(1)} %get-tuple-element.21), channel_id=1, source_target_pairs={{0,752},{1,753},{2,754},{3,755},{4,756},{5,757},{6,758},{7,759},{8... | collective-permute-start | bytes 221192 | tf_op jit(solution)/shard_map/ppermute | solution.py:274
  42.4 5.4 %collective-permute-start.7 = (bf16[6,24,256]{2,1,0:T(8,128)(2,1)S(1)}, bf16[6,24,256]{2,1,0:T(8,128)(2,1)S(1)}, u32[]{:S(2)}, u32[]{:S(2)}) collective-permute-start(bf16[6,24,256]{2,1,0:T(8,128)(2,1)S(1)} %get-tuple-element.22), channel_id=1, source_target_pairs={{0,16},{1,17},{2,18},{3,19},{4,20},{5,21},{6,22},{7,23},{8,24},{9,... | collective-permute-start | bytes 221192 | tf_op jit(solution)/shard_map/ppermute | solution.py:274

commit v3 on v2

--- a/solution.py
+++ b/solution.py
@@ -114,14 +114,14 @@
     return [jnp.where(inside, a, b), jnp.where(inside, b, a)]
 
 
-def flips():
+def flips(mixed):
+    ta, gz = lax.axis_index("ta"), lax.axis_index("gz")
+    return ta % 2 == 1, ((ta + gz) if mixed else gz) % 2 == 1
+
+
+def project_edges(field, u_ref, mixed, z_one, z_two, t_far, t_near):
     ta = lax.axis_index("ta")
-    return ta % 2 == 1, lax.axis_index("gz") % 2 == 1
-
-
-def project_edges(field, u_ref, z_one, z_two, t_far, t_near):
-    ta = lax.axis_index("ta")
-    flip_t, flip_z = flips()
+    flip_t, flip_z = flips(mixed)
     turn_back = jnp.where(ta == 0, -1.0, 1.0).astype(F32)
     turn_on = jnp.where(ta == lax.axis_size("ta") - 1, -1.0, 1.0).astype(F32)
     for j in range(2):
@@ -141,8 +141,8 @@
                     second[at] = jnp.where(flip, bwd[k], fwd[k]).astype(BF16)
 
 
-FIRST_ROUND = (0, 1, 2, 3)
-SECOND_ROUND = (1, 0, 2, 3)
+FIRST_ROUND, FIRST_MIXED = (1, 0, 2, 3), True
+SECOND_ROUND, SECOND_MIXED = (1, 0, 2, 3), False
 
 
 def in_place(order, items):
@@ -150,7 +150,7 @@
 
 
 def first_edges(f_ref, u_ref, *edges):
-    project_edges(lambda k, r, j: get(f_ref, k, r, j), u_ref, *in_place(FIRST_ROUND, edges))
+    project_edges(lambda k, r, j: get(f_ref, k, r, j), u_ref, FIRST_MIXED, *in_place(FIRST_ROUND, edges))
 
 
 def space_hops(f_ref, u_ref, acc_ref):
@@ -194,8 +194,8 @@
                 acc_ref[k, 24 + r * 8 : 32 + r * 8, lanes] = dn_acc.pop((k, r, j))
 
 
-def add_halo(f_ref, u_ref, acc_ref, z_one, z_two, t_far, t_near, out_ref):
-    flip_t, flip_z = flips()
+def add_halo(f_ref, u_ref, acc_ref, mixed, z_one, z_two, t_far, t_near, out_ref):
+    flip_t, flip_z = flips(mixed)
     for j in range(2):
         lanes = slice(j * LANES, (j + 1) * LANES)
         uz = links(u_ref, 2, j)
@@ -225,12 +225,12 @@
 
 
 def finish_and_edges(f_ref, u_ref, acc_ref, h0, h1, h2, h3, out_ref, *edges):
-    add_halo(f_ref, u_ref, acc_ref, *in_place(FIRST_ROUND, (h0, h1, h2, h3)), out_ref)
-    project_edges(lambda k, r, j: get(out_ref, k, r, j), u_ref, *in_place(SECOND_ROUND, edges))
+    add_halo(f_ref, u_ref, acc_ref, FIRST_MIXED, *in_place(FIRST_ROUND, (h0, h1, h2, h3)), out_ref)
+    project_edges(lambda k, r, j: get(out_ref, k, r, j), u_ref, SECOND_MIXED, *in_place(SECOND_ROUND, edges))
 
 
 def finish(f_ref, u_ref, acc_ref, h0, h1, h2, h3, out_ref):
-    add_halo(f_ref, u_ref, acc_ref, *in_place(SECOND_ROUND, (h0, h1, h2, h3)), out_ref)
+    add_halo(f_ref, u_ref, acc_ref, SECOND_MIXED, *in_place(SECOND_ROUND, (h0, h1, h2, h3)), out_ref)
 
 
 SPINOR = pltpu.VMEM((6, 48, 256), BF16)
@@ -250,15 +250,16 @@
     )(*args)
 
 
-def routes(nt, nz):
+def routes(nt, nz, mixed):
     z_one, z_two, t_far, t_near = [], [], [], []
     for t in range(nt):
         for z in range(nz):
             here = t * nz + z
             ahead, behind = t * nz + (z + 1) % nz, t * nz + (z - 1) % nz
             later, earlier = (t + 1) % nt * nz + z, (t - 1) % nt * nz + z
-            z_one.append((here, behind if z % 2 else ahead))
-            z_two.append((here, ahead if z % 2 else behind))
+            flip = ((t + z) if mixed else z) % 2
+            z_one.append((here, behind if flip else ahead))
+            z_two.append((here, ahead if flip else behind))
             t_near.append((here, earlier if t % 2 else later))
             t_far.append((here, later if t % 2 else earlier))
     return z_one, z_two, t_far, t_near
@@ -268,16 +269,16 @@
     nt, nz = lax.axis_size("ta"), lax.axis_size("gz")
     field = source.reshape(2, 4, 3, 12, 256).transpose(0, 2, 1, 3, 4).reshape(6, 48, 256)
     u = gauge_field.reshape(4, 2, 3, 3, 256).transpose(0, 2, 3, 1, 4).reshape(72, 256).astype(F32)
-    pairs = routes(nt, nz)
-
-    def exchange(edges, order):
+
+    def exchange(edges, order, mixed):
+        pairs = routes(nt, nz, mixed)
         return [lax.ppermute(e, ("ta", "gz"), pairs[i]) for i, e in zip(order, edges)]
 
     edges = call(first_edges, "first_edges", [HALF] * 4, field, u)
-    halo = exchange(edges, FIRST_ROUND)
+    halo = exchange(edges, FIRST_ROUND, FIRST_MIXED)
     acc = call(space_hops, "space_hops", SUM, field, u)
     field, *edges = call(finish_and_edges, "finish_and_edges", [SPINOR] + [HALF] * 4, field, u, acc, *halo)
-    halo = exchange(edges, SECOND_ROUND)
+    halo = exchange(edges, SECOND_ROUND, SECOND_MIXED)
     acc = call(space_hops, "space_hops", SUM, field, u)
     field = call(finish, "finish", SPINOR, field, u, acc, *halo)
     return field.reshape(2, 3, 4, 12, 256).transpose(0, 2, 1, 3, 4).reshape(source.shape)

time: 49.2 us -> 48.2 us (0.980)
  the two profiles are of different devices: /device:TPU:6 before, /device:TPU:1 now
where the time goes in v3:
time: 48.2 us; the launch traced here: 47.9 us
  starting transfers between devices  43.2 us (90%)
  Pallas kernels  1.82 us (4%)
  local copies, waits for them, and re-layouts  0.92 us (2%)
  waiting for transfers between devices  0.92 us (2%)
  other arithmetic  0.83 us (2%)
    ppermute x8, starting transfers between devices, exchange(): lax.ppermute(e, ('ta', 'gz'), pairs[i])  43.2 us
    pallas_call x5, Pallas kernels, call(): pl.pallas_call(kernel, out_shape=outs, in_specs=[in_vmem] * len(args), ou...  1.82 us
  transfers between devices with their start and end apart: 8, of which 2 were waited for; matrix products, arithmetic and copies ran while one was open for 0% of the time, Pallas kernels for 2%

profile of v3, /device:TPU:1, one launch (start us, length us, event | category | flops | bytes accessed | tf_op | source)
XLA Modules:
  0.0 47.9 jit_solution(4845705204978290272)
XLA Ops:
  0.0 0.0 copy-start
  0.0 0.8 %convert_bitcast_fusion = f32[4,3,3,2,256]{4,3,2,1,0:T(2,128)S(1)} fusion(bf16[1,1,4,2,3,3,256]{6,3,5,4,2,1,0:T(2,128)(2,1)} %param.3), kind=kLoop, calls=%fused_computation | loop fusion | flops 18432 | bytes 110592 | tf_op jit(solution)/shard_map/convert_element_type | solution.py:271
  0.8 0.1 reshape.22.u_ref
  0.9 0.0 copy-done
  1.0 0.2 first_edges.1
  1.2 8.4 %collective-permute-start = (bf16[6,24,256]{2,1,0:T(8,128)(2,1)S(1)}, bf16[6,24,256]{2,1,0:T(8,128)(2,1)S(1)}, u32[]{:S(2)}, u32[]{:S(2)}) collective-permute-start(bf16[6,24,256]{2,1,0:T(8,128)(2,1)S(1)} %get-tuple-element.14), channel_id=1, source_target_pairs={{0,15},{1,2},{2,1},{3,4},{4,3},{5,6},{6,5},{7,8},{8,7},{9,10},{10,... | collective-permute-start | bytes 221192 | tf_op jit(solution)/shard_map/ppermute | solution.py:275
  9.7 11.6 %collective-permute-start.1 = (bf16[6,24,256]{2,1,0:T(8,128)(2,1)S(1)}, bf16[6,24,256]{2,1,0:T(8,128)(2,1)S(1)}, u32[]{:S(2)}, u32[]{:S(2)}) collective-permute-start(bf16[6,24,256]{2,1,0:T(8,128)(2,1)S(1)} %get-tuple-element.15), channel_id=1, source_target_pairs={{0,1},{1,0},{2,3},{3,2},{4,5},{5,4},{6,7},{7,6},{8,9},{9,8},{10,11... | collective-permute-start | bytes 221192 | tf_op jit(solution)/shard_map/ppermute | solution.py:275
  21.3 3.1 %collective-permute-start.2 = (bf16[6,24,256]{2,1,0:T(8,128)(2,1)S(1)}, bf16[6,24,256]{2,1,0:T(8,128)(2,1)S(1)}, u32[]{:S(2)}, u32[]{:S(2)}) collective-permute-start(bf16[6,24,256]{2,1,0:T(8,128)(2,1)S(1)} %get-tuple-element.16), channel_id=1, source_target_pairs={{0,752},{1,753},{2,754},{3,755},{4,756},{5,757},{6,758},{7,759},{8... | collective-permute-start | bytes 221192 | tf_op jit(solution)/shard_map/ppermute | solution.py:275
  24.4 5.5 %collective-permute-start.3 = (bf16[6,24,256]{2,1,0:T(8,128)(2,1)S(1)}, bf16[6,24,256]{2,1,0:T(8,128)(2,1)S(1)}, u32[]{:S(2)}, u32[]{:S(2)}) collective-permute-start(bf16[6,24,256]{2,1,0:T(8,128)(2,1)S(1)} %get-tuple-element.17), channel_id=1, source_target_pairs={{0,16},{1,17},{2,18},{3,19},{4,20},{5,21},{6,22},{7,23},{8,24},{9,... | collective-permute-start | bytes 221192 | tf_op jit(solution)/shard_map/ppermute | solution.py:275
  29.9 0.4 space_hops.2.acc_ref
  30.3 0.0 collective-permute-done.h0
  30.3 0.0 collective-permute-done.1.h1
  30.3 0.0 collective-permute-done.2.h2
  30.4 0.5 collective-permute-done.3.h3
  30.8 0.5 %finish_and_edges.1 = (bf16[6,48,256]{2,1,0:T(8,128)(2,1)S(1)}, bf16[6,24,256]{2,1,0:T(8,128)(2,1)S(1)}, bf16[6,24,256]{2,1,0:T(8,128)(2,1)S(1)}, bf16[6,24,256]{2,1,0:T(8,128)(2,1)S(1)}, bf16[6,24,256]{2,1,0:T(8,128)(2,1)S(1)}) custom-call(bf16[6,48,256]{2,1,0:T(8,128)(2,1)S(1)} %reshape.19.f_ref, f32[72,256]{1,0:T(8,128)S(1)} %reshape.22.u_ref, ...), custom_call_target="tpu_custom_call" | custom-call | tf_op jit(solution)/shard_map/finish_and_edges/pallas_call | solution.py:244
  31.3 3.1 %collective-permute-start.4 = (bf16[6,24,256]{2,1,0:T(8,128)(2,1)S(1)}, bf16[6,24,256]{2,1,0:T(8,128)(2,1)S(1)}, u32[]{:S(2)}, u32[]{:S(2)}) collective-permute-start(bf16[6,24,256]{2,1,0:T(8,128)(2,1)S(1)} %get-tuple-element.19), channel_id=1, source_target_pairs={{0,15},{1,2},{2,1},{3,4},{4,3},{5,6},{6,5},{7,8},{8,7},{9,10},{10,... | collective-permute-start | bytes 221192 | tf_op jit(solution)/shard_map/ppermute | solution.py:275
  34.4 2.2 %collective-permute-start.5 = (bf16[6,24,256]{2,1,0:T(8,128)(2,1)S(1)}, bf16[6,24,256]{2,1,0:T(8,128)(2,1)S(1)}, u32[]{:S(2)}, u32[]{:S(2)}) collective-permute-start(bf16[6,24,256]{2,1,0:T(8,128)(2,1)S(1)} %get-tuple-element.20), channel_id=1, source_target_pairs={{0,1},{1,0},{2,3},{3,2},{4,5},{5,4},{6,7},{7,6},{8,9},{9,8},{10,11... | collective-permute-start | bytes 221192 | tf_op jit(solution)/shard_map/ppermute | solution.py:275
  36.6 4.3 %collective-permute-start.6 = (bf16[6,24,256]{2,1,0:T(8,128)(2,1)S(1)}, bf16[6,24,256]{2,1,0:T(8,128)(2,1)S(1)}, u32[]{:S(2)}, u32[]{:S(2)}) collective-permute-start(bf16[6,24,256]{2,1,0:T(8,128)(2,1)S(1)} %get-tuple-element.21), channel_id=1, source_target_pairs={{0,752},{1,753},{2,754},{3,755},{4,756},{5,757},{6,758},{7,759},{8... | collective-permute-start | bytes 221192 | tf_op jit(solution)/shard_map/ppermute | solution.py:275
  41.0 4.9 %collective-permute-start.7 = (bf16[6,24,256]{2,1,0:T(8,128)(2,1)S(1)}, bf16[6,24,256]{2,1,0:T(8,128)(2,1)S(1)}, u32[]{:S(2)}, u32[]{:S(2)}) collective-permute-start(bf16[6,24,256]{2,1,0:T(8,128)(2,1)S(1)} %get-tuple-element.22), channel_id=1, source_target_pairs={{0,16},{1,17},{2,18},{3,19},{4,20},{5,21},{6,22},{7,23},{8,24},{9,... | collective-permute-start | bytes 221192 | tf_op jit(solution)/shard_map/ppermute | solution.py:275
  45.9 0.4 space_hops.3.acc_ref
  46.3 0.0 collective-permute-done.4.h0
  46.3 0.0 collective-permute-done.5.h1
  46.3 0.0 collective-permute-done.6.h2
  46.3 0.5 collective-permute-done.7.h3
  46.8 0.3 finish.1
  47.1 0.7 %copy.6 = bf16[1,1,2,4,3,12,256]{6,3,5,4,2,1,0:T(4,128)(2,1)} copy(bf16[1,1,2,4,3,12,256]{6,5,3,4,2,1,0:T(8,128)(2,1)S(1)} %bitcast.11) | data formatting | bytes 294912 | tf_op jit(solution)/shard_map/reshape | solution.py:284
  (3 shorter events, 0.1 us)
Async XLA Ops:
  0.0 0.9 %copy-start = (bf16[1,1,2,4,3,12,256]{6,3,5,4,2,1,0:T(4,128)(2,1)S(1)}, bf16[1,1,2,4,3,12,256]{6,3,5,4,2,1,0:T(4,128)(2,1)}, u32[]{:S(2)}) copy-start(bf16[1,1,2,4,3,12,256]{6,3,5,4,2,1,0:T(4,128)(2,1)} %param.2) | copy-start | bytes 442372
  1.2 29.1 %collective-permute-start = (bf16[6,24,256]{2,1,0:T(8,128)(2,1)S(1)}, bf16[6,24,256]{2,1,0:T(8,128)(2,1)S(1)}, u32[]{:S(2)}, u32[]{:S(2)}) collective-permute-start(bf16[6,24,256]{2,1,0:T(8,128)(2,1)S(1)} %get-tuple-element.14), channel_id=1, source_target_pairs={{0,15},{1,2},{2,1},{3,4},{4,3},{5,6},{6,5},{7,8},{8,7},{9,10},{10,... | collective-permute-start | bytes 221192 | tf_op jit(solution)/shard_map/ppermute | solution.py:275
  9.7 20.7 %collective-permute-start.1 = (bf16[6,24,256]{2,1,0:T(8,128)(2,1)S(1)}, bf16[6,24,256]{2,1,0:T(8,128)(2,1)S(1)}, u32[]{:S(2)}, u32[]{:S(2)}) collective-permute-start(bf16[6,24,256]{2,1,0:T(8,128)(2,1)S(1)} %get-tuple-element.15), channel_id=1, source_target_pairs={{0,1},{1,0},{2,3},{3,2},{4,5},{5,4},{6,7},{7,6},{8,9},{9,8},{10,11... | collective-permute-start | bytes 221192 | tf_op jit(solution)/shard_map/ppermute | solution.py:275
  21.3 9.1 %collective-permute-start.2 = (bf16[6,24,256]{2,1,0:T(8,128)(2,1)S(1)}, bf16[6,24,256]{2,1,0:T(8,128)(2,1)S(1)}, u32[]{:S(2)}, u32[]{:S(2)}) collective-permute-start(bf16[6,24,256]{2,1,0:T(8,128)(2,1)S(1)} %get-tuple-element.16), channel_id=1, source_target_pairs={{0,752},{1,753},{2,754},{3,755},{4,756},{5,757},{6,758},{7,759},{8... | collective-permute-start | bytes 221192 | tf_op jit(solution)/shard_map/ppermute | solution.py:275
  24.4 6.4 %collective-permute-start.3 = (bf16[6,24,256]{2,1,0:T(8,128)(2,1)S(1)}, bf16[6,24,256]{2,1,0:T(8,128)(2,1)S(1)}, u32[]{:S(2)}, u32[]{:S(2)}) collective-permute-start(bf16[6,24,256]{2,1,0:T(8,128)(2,1)S(1)} %get-tuple-element.17), channel_id=1, source_target_pairs={{0,16},{1,17},{2,18},{3,19},{4,20},{5,21},{6,22},{7,23},{8,24},{9,... | collective-permute-start | bytes 221192 | tf_op jit(solution)/shard_map/ppermute | solution.py:275
  31.3 15.0 %collective-permute-start.4 = (bf16[6,24,256]{2,1,0:T(8,128)(2,1)S(1)}, bf16[6,24,256]{2,1,0:T(8,128)(2,1)S(1)}, u32[]{:S(2)}, u32[]{:S(2)}) collective-permute-start(bf16[6,24,256]{2,1,0:T(8,128)(2,1)S(1)} %get-tuple-element.19), channel_id=1, source_target_pairs={{0,15},{1,2},{2,1},{3,4},{4,3},{5,6},{6,5},{7,8},{8,7},{9,10},{10,... | collective-permute-start | bytes 221192 | tf_op jit(solution)/shard_map/ppermute | solution.py:275
  34.4 11.9 %collective-permute-start.5 = (bf16[6,24,256]{2,1,0:T(8,128)(2,1)S(1)}, bf16[6,24,256]{2,1,0:T(8,128)(2,1)S(1)}, u32[]{:S(2)}, u32[]{:S(2)}) collective-permute-start(bf16[6,24,256]{2,1,0:T(8,128)(2,1)S(1)} %get-tuple-element.20), channel_id=1, source_target_pairs={{0,1},{1,0},{2,3},{3,2},{4,5},{5,4},{6,7},{7,6},{8,9},{9,8},{10,11... | collective-permute-start | bytes 221192 | tf_op jit(solution)/shard_map/ppermute | solution.py:275
  36.6 9.7 %collective-permute-start.6 = (bf16[6,24,256]{2,1,0:T(8,128)(2,1)S(1)}, bf16[6,24,256]{2,1,0:T(8,128)(2,1)S(1)}, u32[]{:S(2)}, u32[]{:S(2)}) collective-permute-start(bf16[6,24,256]{2,1,0:T(8,128)(2,1)S(1)} %get-tuple-element.21), channel_id=1, source_target_pairs={{0,752},{1,753},{2,754},{3,755},{4,756},{5,757},{6,758},{7,759},{8... | collective-permute-start | bytes 221192 | tf_op jit(solution)/shard_map/ppermute | solution.py:275
  41.0 5.8 %collective-permute-start.7 = (bf16[6,24,256]{2,1,0:T(8,128)(2,1)S(1)}, bf16[6,24,256]{2,1,0:T(8,128)(2,1)S(1)}, u32[]{:S(2)}, u32[]{:S(2)}) collective-permute-start(bf16[6,24,256]{2,1,0:T(8,128)(2,1)S(1)} %get-tuple-element.22), channel_id=1, source_target_pairs={{0,16},{1,17},{2,18},{3,19},{4,20},{5,21},{6,22},{7,23},{8,24},{9,... | collective-permute-start | bytes 221192 | tf_op jit(solution)/shard_map/ppermute | solution.py:275

commit v4 on v3

--- a/solution.py
+++ b/solution.py
@@ -1,3 +1,5 @@
+import functools
+
 import jax
 import jax.numpy as jnp
 from jax import lax
@@ -147,10 +149,6 @@
 
 def in_place(order, items):
     return [items[order.index(i)] for i in range(4)]
-
-
-def first_edges(f_ref, u_ref, *edges):
-    project_edges(lambda k, r, j: get(f_ref, k, r, j), u_ref, FIRST_MIXED, *in_place(FIRST_ROUND, edges))
 
 
 def space_hops(f_ref, u_ref, acc_ref):
@@ -194,43 +192,56 @@
                 acc_ref[k, 24 + r * 8 : 32 + r * 8, lanes] = dn_acc.pop((k, r, j))
 
 
-def add_halo(f_ref, u_ref, acc_ref, mixed, z_one, z_two, t_far, t_near, out_ref):
-    flip_t, flip_z = flips(mixed)
+def accumulate(mu, r, k6, q, up, dn):
+    lower = spread(mu, r, k6, q)
+    return [a + b for a, b in zip(up, k6)], [a + b for a, b in zip(dn, lower)]
+
+
+def add_z(order, mixed, f_ref, u_ref, acc_ref, h0, h1, base_ref):
+    _, flip_z = flips(mixed)
+    z_one, z_two = (h0, h1) if order.index(0) < order.index(1) else (h1, h0)
     for j in range(2):
         lanes = slice(j * LANES, (j + 1) * LANES)
         uz = links(u_ref, 2, j)
-        ut = links(u_ref, 3, j)
         low = [swap_spins([get(acc_ref, k, 3 + i, j) for i in range(3)]) for k in range(6)]
         for r in range(3):
             up = [get(acc_ref, k, r, j) for k in range(6)]
             dn = [low[k][r] for k in range(6)]
             one = [get(z_one, k, r, j) for k in range(6)]
             two = [get(z_two, k, r, j) for k in range(6)]
+            ahead = times(uz, [jnp.where(flip_z, b, a) for a, b in zip(one, two)], False)
+            behind = [jnp.where(flip_z, a, b) for a, b in zip(one, two)]
+            up, dn = accumulate(2, r, ahead, 1, up, dn)
+            up, dn = accumulate(2, r, behind, -1, up, dn)
+            for k in range(6):
+                for at, hop in ((r, up[k]), (r + 3, dn[k])):
+                    base_ref[k, at * 8 : at * 8 + 8, lanes] = get(f_ref, k, at, j) - HOPPING * hop
+
+
+def add_t(u_ref, base_ref, t_far, t_near, out_ref):
+    flip_t, _ = flips(False)
+    for j in range(2):
+        lanes = slice(j * LANES, (j + 1) * LANES)
+        ut = links(u_ref, 3, j)
+        for r in range(3):
             near = [get(t_near, k, r, j) for k in range(6)]
             far = [get(t_far, k, r, j) for k in range(6)]
-            parts = (
-                (2, times(uz, [jnp.where(flip_z, b, a) for a, b in zip(one, two)], False), 1),
-                (2, [jnp.where(flip_z, a, b) for a, b in zip(one, two)], -1),
-                (3, times(ut, [jnp.where(flip_t, b, a) for a, b in zip(near, far)], False), 1),
-                (3, [jnp.where(flip_t, a, b) for a, b in zip(near, far)], -1),
-            )
-            for mu, k6, q in parts:
-                lower = spread(mu, r, k6, q)
-                up = [a + b for a, b in zip(up, k6)]
-                dn = [a + b for a, b in zip(dn, lower)]
+            up = times(ut, [jnp.where(flip_t, b, a) for a, b in zip(near, far)], False)
+            dn = spread(3, r, up, 1)
+            up, dn = accumulate(3, r, [jnp.where(flip_t, a, b) for a, b in zip(near, far)], -1, up, dn)
             for k in range(6):
                 for at, hop in ((r, up[k]), (r + 3, dn[k])):
-                    value = get(f_ref, k, at, j) - HOPPING * hop
+                    value = get(base_ref, k, at, j) - HOPPING * hop
                     out_ref[k, at * 8 : at * 8 + 8, lanes] = value.astype(BF16)
 
 
-def finish_and_edges(f_ref, u_ref, acc_ref, h0, h1, h2, h3, out_ref, *edges):
-    add_halo(f_ref, u_ref, acc_ref, FIRST_MIXED, *in_place(FIRST_ROUND, (h0, h1, h2, h3)), out_ref)
+def first_edges(f_ref, u_ref, *edges):
+    project_edges(lambda k, r, j: get(f_ref, k, r, j), u_ref, FIRST_MIXED, *in_place(FIRST_ROUND, edges))
+
+
+def add_t_and_edges(u_ref, base_ref, t_far, t_near, out_ref, *edges):
+    add_t(u_ref, base_ref, t_far, t_near, out_ref)
     project_edges(lambda k, r, j: get(out_ref, k, r, j), u_ref, SECOND_MIXED, *in_place(SECOND_ROUND, edges))
-
-
-def finish(f_ref, u_ref, acc_ref, h0, h1, h2, h3, out_ref):
-    add_halo(f_ref, u_ref, acc_ref, SECOND_MIXED, *in_place(SECOND_ROUND, (h0, h1, h2, h3)), out_ref)
 
 
 SPINOR = pltpu.VMEM((6, 48, 256), BF16)
@@ -274,13 +285,19 @@
         pairs = routes(nt, nz, mixed)
         return [lax.ppermute(e, ("ta", "gz"), pairs[i]) for i, e in zip(order, edges)]
 
+    def hops(field, halo, order, mixed):
+        acc = call(space_hops, "space_hops", SUM, field, u)
+        z_halo = [h for i, h in zip(order, halo) if i < 2]
+        base = call(functools.partial(add_z, order, mixed), "add_z", SUM, field, u, acc, *z_halo)
+        _, _, t_far, t_near = in_place(order, halo)
+        return u, base, t_far, t_near
+
     edges = call(first_edges, "first_edges", [HALF] * 4, field, u)
     halo = exchange(edges, FIRST_ROUND, FIRST_MIXED)
-    acc = call(space_hops, "space_hops", SUM, field, u)
-    field, *edges = call(finish_and_edges, "finish_and_edges", [SPINOR] + [HALF] * 4, field, u, acc, *halo)
+    args = hops(field, halo, FIRST_ROUND, FIRST_MIXED)
+    field, *edges = call(add_t_and_edges, "add_t_and_edges", [SPINOR] + [HALF] * 4, *args)
     halo = exchange(edges, SECOND_ROUND, SECOND_MIXED)
-    acc = call(space_hops, "space_hops", SUM, field, u)
-    field = call(finish, "finish", SPINOR, field, u, acc, *halo)
+    field = call(add_t, "add_t", SPINOR, *hops(field, halo, SECOND_ROUND, SECOND_MIXED))
     return field.reshape(2, 3, 4, 12, 256).transpose(0, 2, 1, 3, 4).reshape(source.shape)
 
 

time: 48.2 us -> 47.9 us (level)
    pallas_call x5 -> x7, Pallas kernels: 1.82 us -> 1.87 us  [call(): pl.pallas_call(kernel, out_shape=outs, in_specs=[in_vmem] * len(args), ou...]
where the time goes in v4:
time: 47.9 us; the launch traced here: 47.6 us
  starting transfers between devices  43.2 us (90%)
  Pallas kernels  1.87 us (4%)
  local copies, waits for them, and re-layouts  0.92 us (2%)
  other arithmetic  0.83 us (2%)
  waiting for transfers between devices  0.55 us (1%)
    ppermute x8, starting transfers between devices, exchange(): lax.ppermute(e, ('ta', 'gz'), pairs[i])  43.2 us
    pallas_call x7, Pallas kernels, call(): pl.pallas_call(kernel, out_shape=outs, in_specs=[in_vmem] * len(args), ou...  1.87 us
  transfers between devices with their start and end apart: 8, of which 2 were waited for; matrix products, arithmetic and copies ran while one was open for 0% of the time, Pallas kernels for 2%

profile of v4, /device:TPU:1, one launch (start us, length us, event | category | flops | bytes accessed | tf_op | source)
XLA Modules:
  0.0 47.6 jit_solution(5117022074588786782)
XLA Ops:
  0.0 0.0 copy-start
  0.0 0.8 %convert_bitcast_fusion = f32[4,3,3,2,256]{4,3,2,1,0:T(2,128)S(1)} fusion(bf16[1,1,4,2,3,3,256]{6,3,5,4,2,1,0:T(2,128)(2,1)} %param.3), kind=kLoop, calls=%fused_computation | loop fusion | flops 18432 | bytes 110592 | tf_op jit(solution)/shard_map/convert_element_type | solution.py:282
  0.8 0.1 reshape.22.u_ref
  0.9 0.0 copy-done
  1.0 0.2 first_edges.1
  1.2 8.4 %collective-permute-start = (bf16[6,24,256]{2,1,0:T(8,128)(2,1)S(1)}, bf16[6,24,256]{2,1,0:T(8,128)(2,1)S(1)}, u32[]{:S(2)}, u32[]{:S(2)}) collective-permute-start(bf16[6,24,256]{2,1,0:T(8,128)(2,1)S(1)} %get-tuple-element.14), channel_id=1, source_target_pairs={{0,15},{1,2},{2,1},{3,4},{4,3},{5,6},{6,5},{7,8},{8,7},{9,10},{10,... | collective-permute-start | bytes 221192 | tf_op jit(solution)/shard_map/ppermute | solution.py:286
  9.7 11.6 %collective-permute-start.1 = (bf16[6,24,256]{2,1,0:T(8,128)(2,1)S(1)}, bf16[6,24,256]{2,1,0:T(8,128)(2,1)S(1)}, u32[]{:S(2)}, u32[]{:S(2)}) collective-permute-start(bf16[6,24,256]{2,1,0:T(8,128)(2,1)S(1)} %get-tuple-element.15), channel_id=1, source_target_pairs={{0,1},{1,0},{2,3},{3,2},{4,5},{5,4},{6,7},{7,6},{8,9},{9,8},{10,11... | collective-permute-start | bytes 221192 | tf_op jit(solution)/shard_map/ppermute | solution.py:286
  21.3 3.1 %collective-permute-start.2 = (bf16[6,24,256]{2,1,0:T(8,128)(2,1)S(1)}, bf16[6,24,256]{2,1,0:T(8,128)(2,1)S(1)}, u32[]{:S(2)}, u32[]{:S(2)}) collective-permute-start(bf16[6,24,256]{2,1,0:T(8,128)(2,1)S(1)} %get-tuple-element.16), channel_id=1, source_target_pairs={{0,752},{1,753},{2,754},{3,755},{4,756},{5,757},{6,758},{7,759},{8... | collective-permute-start | bytes 221192 | tf_op jit(solution)/shard_map/ppermute | solution.py:286
  24.4 5.5 %collective-permute-start.3 = (bf16[6,24,256]{2,1,0:T(8,128)(2,1)S(1)}, bf16[6,24,256]{2,1,0:T(8,128)(2,1)S(1)}, u32[]{:S(2)}, u32[]{:S(2)}) collective-permute-start(bf16[6,24,256]{2,1,0:T(8,128)(2,1)S(1)} %get-tuple-element.17), channel_id=1, source_target_pairs={{0,16},{1,17},{2,18},{3,19},{4,20},{5,21},{6,22},{7,23},{8,24},{9,... | collective-permute-start | bytes 221192 | tf_op jit(solution)/shard_map/ppermute | solution.py:286
  29.9 0.4 space_hops.2.acc_ref
  30.3 0.0 collective-permute-done.h0
  30.3 0.0 collective-permute-done.1.h1
  30.3 0.2 add_z.2.base_ref
  30.5 0.0 collective-permute-done.2.t_far
  30.5 0.3 collective-permute-done.3.t_near
  30.8 0.3 add_t_and_edges.1
  31.2 3.3 %collective-permute-start.4 = (bf16[6,24,256]{2,1,0:T(8,128)(2,1)S(1)}, bf16[6,24,256]{2,1,0:T(8,128)(2,1)S(1)}, u32[]{:S(2)}, u32[]{:S(2)}) collective-permute-start(bf16[6,24,256]{2,1,0:T(8,128)(2,1)S(1)} %get-tuple-element.19), channel_id=1, source_target_pairs={{0,15},{1,2},{2,1},{3,4},{4,3},{5,6},{6,5},{7,8},{8,7},{9,10},{10,... | collective-permute-start | bytes 221192 | tf_op jit(solution)/shard_map/ppermute | solution.py:286
  34.5 2.0 %collective-permute-start.5 = (bf16[6,24,256]{2,1,0:T(8,128)(2,1)S(1)}, bf16[6,24,256]{2,1,0:T(8,128)(2,1)S(1)}, u32[]{:S(2)}, u32[]{:S(2)}) collective-permute-start(bf16[6,24,256]{2,1,0:T(8,128)(2,1)S(1)} %get-tuple-element.20), channel_id=1, source_target_pairs={{0,1},{1,0},{2,3},{3,2},{4,5},{5,4},{6,7},{7,6},{8,9},{9,8},{10,11... | collective-permute-start | bytes 221192 | tf_op jit(solution)/shard_map/ppermute | solution.py:286
  36.5 4.3 %collective-permute-start.6 = (bf16[6,24,256]{2,1,0:T(8,128)(2,1)S(1)}, bf16[6,24,256]{2,1,0:T(8,128)(2,1)S(1)}, u32[]{:S(2)}, u32[]{:S(2)}) collective-permute-start(bf16[6,24,256]{2,1,0:T(8,128)(2,1)S(1)} %get-tuple-element.21), channel_id=1, source_target_pairs={{0,752},{1,753},{2,754},{3,755},{4,756},{5,757},{6,758},{7,759},{8... | collective-permute-start | bytes 221192 | tf_op jit(solution)/shard_map/ppermute | solution.py:286
  40.8 4.9 %collective-permute-start.7 = (bf16[6,24,256]{2,1,0:T(8,128)(2,1)S(1)}, bf16[6,24,256]{2,1,0:T(8,128)(2,1)S(1)}, u32[]{:S(2)}, u32[]{:S(2)}) collective-permute-start(bf16[6,24,256]{2,1,0:T(8,128)(2,1)S(1)} %get-tuple-element.22), channel_id=1, source_target_pairs={{0,16},{1,17},{2,18},{3,19},{4,20},{5,21},{6,22},{7,23},{8,24},{9,... | collective-permute-start | bytes 221192 | tf_op jit(solution)/shard_map/ppermute | solution.py:286
  45.8 0.4 space_hops.3.acc_ref
  46.2 0.0 collective-permute-done.4.h0
  46.2 0.0 collective-permute-done.5.h1
  46.2 0.2 add_z.3.base_ref
  46.4 0.0 collective-permute-done.6.t_far
  46.4 0.3 collective-permute-done.7.t_near
  46.6 0.1 add_t.1
  46.8 0.7 %copy.6 = bf16[1,1,2,4,3,12,256]{6,3,5,4,2,1,0:T(4,128)(2,1)} copy(bf16[1,1,2,4,3,12,256]{6,5,3,4,2,1,0:T(8,128)(2,1)S(1)} %bitcast.11) | data formatting | bytes 294912 | tf_op jit(solution)/shard_map/reshape | solution.py:301
  (3 shorter events, 0.1 us)
Async XLA Ops:
  0.0 0.9 %copy-start = (bf16[1,1,2,4,3,12,256]{6,3,5,4,2,1,0:T(4,128)(2,1)S(1)}, bf16[1,1,2,4,3,12,256]{6,3,5,4,2,1,0:T(4,128)(2,1)}, u32[]{:S(2)}) copy-start(bf16[1,1,2,4,3,12,256]{6,3,5,4,2,1,0:T(4,128)(2,1)} %param.2) | copy-start | bytes 442372
  1.2 29.1 %collective-permute-start = (bf16[6,24,256]{2,1,0:T(8,128)(2,1)S(1)}, bf16[6,24,256]{2,1,0:T(8,128)(2,1)S(1)}, u32[]{:S(2)}, u32[]{:S(2)}) collective-permute-start(bf16[6,24,256]{2,1,0:T(8,128)(2,1)S(1)} %get-tuple-element.14), channel_id=1, source_target_pairs={{0,15},{1,2},{2,1},{3,4},{4,3},{5,6},{6,5},{7,8},{8,7},{9,10},{10,... | collective-permute-start | bytes 221192 | tf_op jit(solution)/shard_map/ppermute | solution.py:286
  9.7 20.7 %collective-permute-start.1 = (bf16[6,24,256]{2,1,0:T(8,128)(2,1)S(1)}, bf16[6,24,256]{2,1,0:T(8,128)(2,1)S(1)}, u32[]{:S(2)}, u32[]{:S(2)}) collective-permute-start(bf16[6,24,256]{2,1,0:T(8,128)(2,1)S(1)} %get-tuple-element.15), channel_id=1, source_target_pairs={{0,1},{1,0},{2,3},{3,2},{4,5},{5,4},{6,7},{7,6},{8,9},{9,8},{10,11... | collective-permute-start | bytes 221192 | tf_op jit(solution)/shard_map/ppermute | solution.py:286
  21.3 9.2 %collective-permute-start.2 = (bf16[6,24,256]{2,1,0:T(8,128)(2,1)S(1)}, bf16[6,24,256]{2,1,0:T(8,128)(2,1)S(1)}, u32[]{:S(2)}, u32[]{:S(2)}) collective-permute-start(bf16[6,24,256]{2,1,0:T(8,128)(2,1)S(1)} %get-tuple-element.16), channel_id=1, source_target_pairs={{0,752},{1,753},{2,754},{3,755},{4,756},{5,757},{6,758},{7,759},{8... | collective-permute-start | bytes 221192 | tf_op jit(solution)/shard_map/ppermute | solution.py:286
  24.4 6.4 %collective-permute-start.3 = (bf16[6,24,256]{2,1,0:T(8,128)(2,1)S(1)}, bf16[6,24,256]{2,1,0:T(8,128)(2,1)S(1)}, u32[]{:S(2)}, u32[]{:S(2)}) collective-permute-start(bf16[6,24,256]{2,1,0:T(8,128)(2,1)S(1)} %get-tuple-element.17), channel_id=1, source_target_pairs={{0,16},{1,17},{2,18},{3,19},{4,20},{5,21},{6,22},{7,23},{8,24},{9,... | collective-permute-start | bytes 221192 | tf_op jit(solution)/shard_map/ppermute | solution.py:286
  31.2 15.0 %collective-permute-start.4 = (bf16[6,24,256]{2,1,0:T(8,128)(2,1)S(1)}, bf16[6,24,256]{2,1,0:T(8,128)(2,1)S(1)}, u32[]{:S(2)}, u32[]{:S(2)}) collective-permute-start(bf16[6,24,256]{2,1,0:T(8,128)(2,1)S(1)} %get-tuple-element.19), channel_id=1, source_target_pairs={{0,15},{1,2},{2,1},{3,4},{4,3},{5,6},{6,5},{7,8},{8,7},{9,10},{10,... | collective-permute-start | bytes 221192 | tf_op jit(solution)/shard_map/ppermute | solution.py:286
  34.5 11.7 %collective-permute-start.5 = (bf16[6,24,256]{2,1,0:T(8,128)(2,1)S(1)}, bf16[6,24,256]{2,1,0:T(8,128)(2,1)S(1)}, u32[]{:S(2)}, u32[]{:S(2)}) collective-permute-start(bf16[6,24,256]{2,1,0:T(8,128)(2,1)S(1)} %get-tuple-element.20), channel_id=1, source_target_pairs={{0,1},{1,0},{2,3},{3,2},{4,5},{5,4},{6,7},{7,6},{8,9},{9,8},{10,11... | collective-permute-start | bytes 221192 | tf_op jit(solution)/shard_map/ppermute | solution.py:286
  36.5 9.9 %collective-permute-start.6 = (bf16[6,24,256]{2,1,0:T(8,128)(2,1)S(1)}, bf16[6,24,256]{2,1,0:T(8,128)(2,1)S(1)}, u32[]{:S(2)}, u32[]{:S(2)}) collective-permute-start(bf16[6,24,256]{2,1,0:T(8,128)(2,1)S(1)} %get-tuple-element.21), channel_id=1, source_target_pairs={{0,752},{1,753},{2,754},{3,755},{4,756},{5,757},{6,758},{7,759},{8... | collective-permute-start | bytes 221192 | tf_op jit(solution)/shard_map/ppermute | solution.py:286
  40.8 5.8 %collective-permute-start.7 = (bf16[6,24,256]{2,1,0:T(8,128)(2,1)S(1)}, bf16[6,24,256]{2,1,0:T(8,128)(2,1)S(1)}, u32[]{:S(2)}, u32[]{:S(2)}) collective-permute-start(bf16[6,24,256]{2,1,0:T(8,128)(2,1)S(1)} %get-tuple-element.22), channel_id=1, source_target_pairs={{0,16},{1,17},{2,18},{3,19},{4,20},{5,21},{6,22},{7,23},{8,24},{9,... | collective-permute-start | bytes 221192 | tf_op jit(solution)/shard_map/ppermute | solution.py:286

commit v5 on v4

--- a/solution.py
+++ b/solution.py
@@ -116,39 +116,60 @@
     return [jnp.where(inside, a, b), jnp.where(inside, b, a)]
 
 
-def flips(mixed):
-    ta, gz = lax.axis_index("ta"), lax.axis_index("gz")
-    return ta % 2 == 1, ((ta + gz) if mixed else gz) % 2 == 1
-
-
-def project_edges(field, u_ref, mixed, z_one, z_two, t_far, t_near):
+Z_AHEAD, Z_BEHIND, T_NEAR, T_FAR = range(4)
+FIRST = ((2, 1, 3, 0), (1, 2, 3, 0), (2, 1, 0, 3), (1, 2, 0, 3), (1, 2, 3, 0), (2, 1, 3, 0), (1, 2, 3, 0), (2, 1, 3, 0))
+SECOND = ((1, 0, 3, 2), (1, 2, 0, 3), (2, 3, 0, 1), (1, 2, 0, 3), (1, 2, 3, 0), (3, 1, 2, 0), (1, 2, 3, 0), (0, 2, 1, 3))
+
+
+def arrivals(table):
+    def row(p, z):
+        other = 4 * (1 - p) + z
+        return table[4 * p + (z + 1) % 4][Z_BEHIND], table[4 * p + (z - 1) % 4][Z_AHEAD], table[other][T_NEAR], table[other][T_FAR]
+
+    return tuple(row(p, z) for p in range(2) for z in range(4))
+
+
+def row_flags():
+    row = 4 * (lax.axis_index("ta") % 2) + lax.axis_index("gz") % 4
+    return [row == i for i in range(8)]
+
+
+def pick(flags, which, tiles):
+    kinds = sorted(set(which), key=which.count)
+    out = tiles[kinds[-1]]
+    for kind in kinds[:-1]:
+        holds = functools.reduce(jnp.logical_or, [f for f, w in zip(flags, which) if w == kind])
+        out = [jnp.where(holds, a, b) for a, b in zip(tiles[kind], out)]
+    return out
+
+
+def project_edges(field, u_ref, table, edges):
     ta = lax.axis_index("ta")
-    flip_t, flip_z = flips(mixed)
+    flags = row_flags()
+    flip = ta % 2 == 1
     turn_back = jnp.where(ta == 0, -1.0, 1.0).astype(F32)
     turn_on = jnp.where(ta == lax.axis_size("ta") - 1, -1.0, 1.0).astype(F32)
     for j in range(2):
-        for mu, flip, first, second in ((2, flip_z, z_one, z_two), (3, flip_t, t_near, t_far)):
-            u = links(u_ref, mu, j)
-            for r in range(3):
-                up = [field(k, r, j) for k in range(6)]
-                dn = [field(k, r + 3, j) for k in range(6)]
-                fwd = mix(mu, r, up, dn, 1)
-                bwd = times(u, mix(mu, r, up, dn, -1), True)
-                if mu == 3:
-                    fwd = [v * turn_back for v in fwd]
-                    bwd = [v * turn_on for v in bwd]
+        uz, ut = links(u_ref, 2, j), links(u_ref, 3, j)
+        for r in range(3):
+            up = [field(k, r, j) for k in range(6)]
+            dn = [field(k, r + 3, j) for k in range(6)]
+            z_fwd = mix(2, r, up, dn, 1)
+            z_bwd = times(uz, mix(2, r, up, dn, -1), True)
+            t_fwd = [v * turn_back for v in mix(3, r, up, dn, 1)]
+            t_bwd = [v * turn_on for v in times(ut, mix(3, r, up, dn, -1), True)]
+            near = [jnp.where(flip, a, b) for a, b in zip(t_fwd, t_bwd)]
+            far = [jnp.where(flip, b, a) for a, b in zip(t_fwd, t_bwd)]
+            for swap, ref in enumerate(edges):
+                sent = pick(flags, [row.index(swap) for row in table], [z_bwd, z_fwd, near, far])
                 for k in range(6):
-                    at = (k, slice(r * 8, r * 8 + 8), slice(j * LANES, (j + 1) * LANES))
-                    first[at] = jnp.where(flip, fwd[k], bwd[k]).astype(BF16)
-                    second[at] = jnp.where(flip, bwd[k], fwd[k]).astype(BF16)
-
-
-FIRST_ROUND, FIRST_MIXED = (1, 0, 2, 3), True
-SECOND_ROUND, SECOND_MIXED = (1, 0, 2, 3), False
-
-
-def in_place(order, items):
-    return [items[order.index(i)] for i in range(4)]
+                    ref[k, r * 8 : r * 8 + 8, j * LANES : (j + 1) * LANES] = sent[k].astype(BF16)
+
+
+def received(flags, table, kind, refs, r, j):
+    which = [row[kind] for row in arrivals(table)]
+    tiles = {swap: [get(refs[swap], k, r, j) for k in range(6)] for swap in set(which)}
+    return pick(flags, which, tiles)
 
 
 def space_hops(f_ref, u_ref, acc_ref):
@@ -197,9 +218,18 @@
     return [a + b for a, b in zip(up, k6)], [a + b for a, b in zip(dn, lower)]
 
 
-def add_z(order, mixed, f_ref, u_ref, acc_ref, h0, h1, base_ref):
-    _, flip_z = flips(mixed)
-    z_one, z_two = (h0, h1) if order.index(0) < order.index(1) else (h1, h0)
+def swaps_of(table, *kinds):
+    return sorted({row[kind] for row in arrivals(table) for kind in kinds})
+
+
+def z_swaps(table):
+    return list(range(max(swaps_of(table, Z_AHEAD, Z_BEHIND)) + 1))
+
+
+def add_z(table, f_ref, u_ref, acc_ref, *refs):
+    *halo, base_ref = refs
+    halo = dict(zip(z_swaps(table), halo))
+    flags = row_flags()
     for j in range(2):
         lanes = slice(j * LANES, (j + 1) * LANES)
         uz = links(u_ref, 2, j)
@@ -207,28 +237,28 @@
         for r in range(3):
             up = [get(acc_ref, k, r, j) for k in range(6)]
             dn = [low[k][r] for k in range(6)]
-            one = [get(z_one, k, r, j) for k in range(6)]
-            two = [get(z_two, k, r, j) for k in range(6)]
-            ahead = times(uz, [jnp.where(flip_z, b, a) for a, b in zip(one, two)], False)
-            behind = [jnp.where(flip_z, a, b) for a, b in zip(one, two)]
+            ahead = times(uz, received(flags, table, Z_AHEAD, halo, r, j), False)
             up, dn = accumulate(2, r, ahead, 1, up, dn)
-            up, dn = accumulate(2, r, behind, -1, up, dn)
+            up, dn = accumulate(2, r, received(flags, table, Z_BEHIND, halo, r, j), -1, up, dn)
             for k in range(6):
                 for at, hop in ((r, up[k]), (r + 3, dn[k])):
                     base_ref[k, at * 8 : at * 8 + 8, lanes] = get(f_ref, k, at, j) - HOPPING * hop
 
 
-def add_t(u_ref, base_ref, t_far, t_near, out_ref):
-    flip_t, _ = flips(False)
+def add_t(table, u_ref, base_ref, *refs):
+    *halo, out_ref = refs
+    halo = dict(zip(swaps_of(table, T_NEAR, T_FAR), halo))
+    flags = row_flags()
+    flip = lax.axis_index("ta") % 2 == 1
     for j in range(2):
         lanes = slice(j * LANES, (j + 1) * LANES)
         ut = links(u_ref, 3, j)
         for r in range(3):
-            near = [get(t_near, k, r, j) for k in range(6)]
-            far = [get(t_far, k, r, j) for k in range(6)]
-            up = times(ut, [jnp.where(flip_t, b, a) for a, b in zip(near, far)], False)
+            near = received(flags, table, T_NEAR, halo, r, j)
+            far = received(flags, table, T_FAR, halo, r, j)
+            up = times(ut, [jnp.where(flip, b, a) for a, b in zip(near, far)], False)
             dn = spread(3, r, up, 1)
-            up, dn = accumulate(3, r, [jnp.where(flip_t, a, b) for a, b in zip(near, far)], -1, up, dn)
+            up, dn = accumulate(3, r, [jnp.where(flip, a, b) for a, b in zip(near, far)], -1, up, dn)
             for k in range(6):
                 for at, hop in ((r, up[k]), (r + 3, dn[k])):
                     value = get(base_ref, k, at, j) - HOPPING * hop
@@ -236,12 +266,14 @@
 
 
 def first_edges(f_ref, u_ref, *edges):
-    project_edges(lambda k, r, j: get(f_ref, k, r, j), u_ref, FIRST_MIXED, *in_place(FIRST_ROUND, edges))
-
-
-def add_t_and_edges(u_ref, base_ref, t_far, t_near, out_ref, *edges):
-    add_t(u_ref, base_ref, t_far, t_near, out_ref)
-    project_edges(lambda k, r, j: get(out_ref, k, r, j), u_ref, SECOND_MIXED, *in_place(SECOND_ROUND, edges))
+    project_edges(lambda k, r, j: get(f_ref, k, r, j), u_ref, FIRST, edges)
+
+
+def add_t_and_edges(u_ref, base_ref, *refs):
+    count = len(swaps_of(FIRST, T_NEAR, T_FAR))
+    out_ref = refs[count]
+    add_t(FIRST, u_ref, base_ref, *refs[: count + 1])
+    project_edges(lambda k, r, j: get(out_ref, k, r, j), u_ref, SECOND, refs[count + 1 :])
 
 
 SPINOR = pltpu.VMEM((6, 48, 256), BF16)
@@ -261,19 +293,16 @@
     )(*args)
 
 
-def routes(nt, nz, mixed):
-    z_one, z_two, t_far, t_near = [], [], [], []
+def routes(nt, nz, table):
+    out = [[], [], [], []]
     for t in range(nt):
         for z in range(nz):
-            here = t * nz + z
-            ahead, behind = t * nz + (z + 1) % nz, t * nz + (z - 1) % nz
-            later, earlier = (t + 1) % nt * nz + z, (t - 1) % nt * nz + z
-            flip = ((t + z) if mixed else z) % 2
-            z_one.append((here, behind if flip else ahead))
-            z_two.append((here, ahead if flip else behind))
-            t_near.append((here, earlier if t % 2 else later))
-            t_far.append((here, later if t % 2 else earlier))
-    return z_one, z_two, t_far, t_near
+            for kind, swap in enumerate(table[4 * (t % 2) + z % 4]):
+                partner_z = z + 1 if kind == Z_AHEAD else z - 1 if kind == Z_BEHIND else z
+                later = (kind == T_NEAR) == (t % 2 == 0)
+                partner_t = t if kind in (Z_AHEAD, Z_BEHIND) else t + 1 if later else t - 1
+                out[swap].append((t * nz + z, partner_t % nt * nz + partner_z % nz))
+    return out
 
 
 def body(source, gauge_field):
@@ -281,23 +310,19 @@
     field = source.reshape(2, 4, 3, 12, 256).transpose(0, 2, 1, 3, 4).reshape(6, 48, 256)
     u = gauge_field.reshape(4, 2, 3, 3, 256).transpose(0, 2, 3, 1, 4).reshape(72, 256).astype(F32)
 
-    def exchange(edges, order, mixed):
-        pairs = routes(nt, nz, mixed)
-        return [lax.ppermute(e, ("ta", "gz"), pairs[i]) for i, e in zip(order, edges)]
-
-    def hops(field, halo, order, mixed):
+    def exchange(edges, table):
+        return [lax.ppermute(e, ("ta", "gz"), p) for e, p in zip(edges, routes(nt, nz, table))]
+
+    def hops(field, halo, table):
         acc = call(space_hops, "space_hops", SUM, field, u)
-        z_halo = [h for i, h in zip(order, halo) if i < 2]
-        base = call(functools.partial(add_z, order, mixed), "add_z", SUM, field, u, acc, *z_halo)
-        _, _, t_far, t_near = in_place(order, halo)
-        return u, base, t_far, t_near
-
-    edges = call(first_edges, "first_edges", [HALF] * 4, field, u)
-    halo = exchange(edges, FIRST_ROUND, FIRST_MIXED)
-    args = hops(field, halo, FIRST_ROUND, FIRST_MIXED)
-    field, *edges = call(add_t_and_edges, "add_t_and_edges", [SPINOR] + [HALF] * 4, *args)
-    halo = exchange(edges, SECOND_ROUND, SECOND_MIXED)
-    field = call(add_t, "add_t", SPINOR, *hops(field, halo, SECOND_ROUND, SECOND_MIXED))
+        z_halo = [halo[i] for i in z_swaps(table)]
+        base = call(functools.partial(add_z, table), "add_z", SUM, field, u, acc, *z_halo)
+        return u, base, *[halo[i] for i in swaps_of(table, T_NEAR, T_FAR)]
+
+    halo = exchange(call(first_edges, "first_edges", [HALF] * 4, field, u), FIRST)
+    field, *edges = call(add_t_and_edges, "add_t_and_edges", [SPINOR] + [HALF] * 4, *hops(field, halo, FIRST))
+    halo = exchange(edges, SECOND)
+    field = call(functools.partial(add_t, SECOND), "add_t", SPINOR, *hops(field, halo, SECOND))
     return field.reshape(2, 3, 4, 12, 256).transpose(0, 2, 1, 3, 4).reshape(source.shape)
 
 

time: 47.9 us -> 47.8 us (level)
  the two profiles are of different devices: /device:TPU:1 before, /device:TPU:198 now
where the time goes in v5:
time: 47.8 us; the launch traced here: 47.4 us
  starting transfers between devices  38.3 us (80%)
  waiting for transfers between devices  5.2 us (11%)
  Pallas kernels  2.04 us (4%)
  local copies, waits for them, and re-layouts  0.92 us (2%)
  other arithmetic  0.83 us (2%)
    ppermute x8, starting transfers between devices, exchange(): lax.ppermute(e, ('ta', 'gz'), p)  38.3 us
    ppermute x8, waiting for transfers between devices, exchange(): lax.ppermute(e, ('ta', 'gz'), p)  5.2 us
    pallas_call x7, Pallas kernels, call(): pl.pallas_call(kernel, out_shape=outs, in_specs=[in_vmem] * len(args), ou...  2.04 us
  transfers between devices with their start and end apart: 8, of which 2 were waited for; matrix products, arithmetic and copies ran while one was open for 0% of the time, Pallas kernels for 2%

profile of v5, /device:TPU:198, one launch (start us, length us, event | category | flops | bytes accessed | tf_op | source)
XLA Modules:
  0.0 47.4 jit_solution(14534071579511527794)
XLA Ops:
  0.0 0.0 copy-start
  0.0 0.8 %convert_bitcast_fusion = f32[4,3,3,2,256]{4,3,2,1,0:T(2,128)S(1)} fusion(bf16[1,1,4,2,3,3,256]{6,3,5,4,2,1,0:T(2,128)(2,1)} %param.3), kind=kLoop, calls=%fused_computation | loop fusion | flops 18432 | bytes 110592 | tf_op jit(solution)/shard_map/convert_element_type | solution.py:311
  0.8 0.1 reshape.22.u_ref
  0.9 0.0 copy-done
  1.0 0.2 first_edges.1
  1.2 9.6 %collective-permute-start = (bf16[6,24,256]{2,1,0:T(8,128)(2,1)S(1)}, bf16[6,24,256]{2,1,0:T(8,128)(2,1)S(1)}, u32[]{:S(2)}, u32[]{:S(2)}) collective-permute-start(bf16[6,24,256]{2,1,0:T(8,128)(2,1)S(1)} %get-tuple-element.14), channel_id=1, source_target_pairs={{0,752},{1,753},{2,18},{3,19},{4,756},{5,757},{6,22},{7,23},{8,760... | collective-permute-start | bytes 221192 | tf_op jit(solution)/shard_map/ppermute | solution.py:314
  10.9 1.9 %collective-permute-start.1 = (bf16[6,24,256]{2,1,0:T(8,128)(2,1)S(1)}, bf16[6,24,256]{2,1,0:T(8,128)(2,1)S(1)}, u32[]{:S(2)}, u32[]{:S(2)}) collective-permute-start(bf16[6,24,256]{2,1,0:T(8,128)(2,1)S(1)} %get-tuple-element.15), channel_id=1, source_target_pairs={{0,15},{1,2},{2,1},{3,4},{4,3},{5,6},{6,5},{7,8},{8,7},{9,10},{10,... | collective-permute-start | bytes 221192 | tf_op jit(solution)/shard_map/ppermute | solution.py:314
  12.8 4.9 %collective-permute-start.2 = (bf16[6,24,256]{2,1,0:T(8,128)(2,1)S(1)}, bf16[6,24,256]{2,1,0:T(8,128)(2,1)S(1)}, u32[]{:S(2)}, u32[]{:S(2)}) collective-permute-start(bf16[6,24,256]{2,1,0:T(8,128)(2,1)S(1)} %get-tuple-element.16), channel_id=1, source_target_pairs={{0,1},{1,0},{2,3},{3,2},{4,5},{5,4},{6,7},{7,6},{8,9},{9,8},{10,11... | collective-permute-start | bytes 221192 | tf_op jit(solution)/shard_map/ppermute | solution.py:314
  17.7 3.3 %collective-permute-start.3 = (bf16[6,24,256]{2,1,0:T(8,128)(2,1)S(1)}, bf16[6,24,256]{2,1,0:T(8,128)(2,1)S(1)}, u32[]{:S(2)}, u32[]{:S(2)}) collective-permute-start(bf16[6,24,256]{2,1,0:T(8,128)(2,1)S(1)} %get-tuple-element.17), channel_id=1, source_target_pairs={{0,16},{1,17},{2,754},{3,755},{4,20},{5,21},{6,758},{7,759},{8,24}... | collective-permute-start | bytes 221192 | tf_op jit(solution)/shard_map/ppermute | solution.py:314
  21.0 0.4 space_hops.2.acc_ref
  21.4 0.0 collective-permute-done.refs_0_
  21.4 0.0 collective-permute-done.1.refs_1_
  21.4 0.4 collective-permute-done.2.refs_2_
  21.9 0.2 add_z.2.base_ref
  22.1 0.0 collective-permute-done.3.refs_1_
  22.1 0.4 add_t_and_edges.1
  22.5 2.1 %collective-permute-start.4 = (bf16[6,24,256]{2,1,0:T(8,128)(2,1)S(1)}, bf16[6,24,256]{2,1,0:T(8,128)(2,1)S(1)}, u32[]{:S(2)}, u32[]{:S(2)}) collective-permute-start(bf16[6,24,256]{2,1,0:T(8,128)(2,1)S(1)} %get-tuple-element.19), channel_id=1, source_target_pairs={{0,15},{1,17},{2,18},{3,19},{4,3},{5,21},{6,22},{7,23},{8,7},{9,25... | collective-permute-start | bytes 221192 | tf_op jit(solution)/shard_map/ppermute | solution.py:314
  24.6 7.1 %collective-permute-start.5 = (bf16[6,24,256]{2,1,0:T(8,128)(2,1)S(1)}, bf16[6,24,256]{2,1,0:T(8,128)(2,1)S(1)}, u32[]{:S(2)}, u32[]{:S(2)}) collective-permute-start(bf16[6,24,256]{2,1,0:T(8,128)(2,1)S(1)} %get-tuple-element.20), channel_id=1, source_target_pairs={{0,1},{1,2},{2,754},{3,4},{4,5},{5,6},{6,758},{7,8},{8,9},{9,10},{... | collective-permute-start | bytes 221192 | tf_op jit(solution)/shard_map/ppermute | solution.py:314
  31.6 2.8 %collective-permute-start.6 = (bf16[6,24,256]{2,1,0:T(8,128)(2,1)S(1)}, bf16[6,24,256]{2,1,0:T(8,128)(2,1)S(1)}, u32[]{:S(2)}, u32[]{:S(2)}) collective-permute-start(bf16[6,24,256]{2,1,0:T(8,128)(2,1)S(1)} %get-tuple-element.21), channel_id=1, source_target_pairs={{0,752},{1,0},{2,3},{3,2},{4,756},{5,4},{6,7},{7,6},{8,760},{9,8},... | collective-permute-start | bytes 221192 | tf_op jit(solution)/shard_map/ppermute | solution.py:314
  34.5 6.5 %collective-permute-start.7 = (bf16[6,24,256]{2,1,0:T(8,128)(2,1)S(1)}, bf16[6,24,256]{2,1,0:T(8,128)(2,1)S(1)}, u32[]{:S(2)}, u32[]{:S(2)}) collective-permute-start(bf16[6,24,256]{2,1,0:T(8,128)(2,1)S(1)} %get-tuple-element.22), channel_id=1, source_target_pairs={{0,16},{1,753},{2,1},{3,755},{4,20},{5,757},{6,5},{7,759},{8,24},{... | collective-permute-start | bytes 221192 | tf_op jit(solution)/shard_map/ppermute | solution.py:314
  41.0 0.4 space_hops.3.acc_ref
  41.4 0.0 collective-permute-done.4.refs_0_
  41.4 0.0 collective-permute-done.5.refs_1_
  41.5 0.0 collective-permute-done.6.refs_2_
  41.5 4.7 %collective-permute-done.7.refs_3_ = bf16[6,24,256]{2,1,0:T(8,128)(2,1)S(1)} collective-permute-done((bf16[6,24,256]{2,1,0:T(8,128)(2,1)S(1)}, bf16[6,24,256]{2,1,0:T(8,128)(2,1)S(1)}, u32[]{:S(2)}, u32[]{:S(2)}) %collective-permute-start.7) | collective-permute-done | bytes 73760 | tf_op jit(solution)/shard_map/ppermute | solution.py:314
  46.2 0.2 add_z.3.base_ref
  46.4 0.2 add_t.1
  46.7 0.7 %copy.6 = bf16[1,1,2,4,3,12,256]{6,3,5,4,2,1,0:T(4,128)(2,1)} copy(bf16[1,1,2,4,3,12,256]{6,5,3,4,2,1,0:T(8,128)(2,1)S(1)} %bitcast.11) | data formatting | bytes 294912 | tf_op jit(solution)/shard_map/reshape | solution.py:326
  (3 shorter events, 0.1 us)
Async XLA Ops:
  0.0 0.9 %copy-start = (bf16[1,1,2,4,3,12,256]{6,3,5,4,2,1,0:T(4,128)(2,1)S(1)}, bf16[1,1,2,4,3,12,256]{6,3,5,4,2,1,0:T(4,128)(2,1)}, u32[]{:S(2)}) copy-start(bf16[1,1,2,4,3,12,256]{6,3,5,4,2,1,0:T(4,128)(2,1)} %param.2) | copy-start | bytes 442372
  1.2 20.2 %collective-permute-start = (bf16[6,24,256]{2,1,0:T(8,128)(2,1)S(1)}, bf16[6,24,256]{2,1,0:T(8,128)(2,1)S(1)}, u32[]{:S(2)}, u32[]{:S(2)}) collective-permute-start(bf16[6,24,256]{2,1,0:T(8,128)(2,1)S(1)} %get-tuple-element.14), channel_id=1, source_target_pairs={{0,752},{1,753},{2,18},{3,19},{4,756},{5,757},{6,22},{7,23},{8,760... | collective-permute-start | bytes 221192 | tf_op jit(solution)/shard_map/ppermute | solution.py:314
  10.9 10.6 %collective-permute-start.1 = (bf16[6,24,256]{2,1,0:T(8,128)(2,1)S(1)}, bf16[6,24,256]{2,1,0:T(8,128)(2,1)S(1)}, u32[]{:S(2)}, u32[]{:S(2)}) collective-permute-start(bf16[6,24,256]{2,1,0:T(8,128)(2,1)S(1)} %get-tuple-element.15), channel_id=1, source_target_pairs={{0,15},{1,2},{2,1},{3,4},{4,3},{5,6},{6,5},{7,8},{8,7},{9,10},{10,... | collective-permute-start | bytes 221192 | tf_op jit(solution)/shard_map/ppermute | solution.py:314
  12.8 9.1 %collective-permute-start.2 = (bf16[6,24,256]{2,1,0:T(8,128)(2,1)S(1)}, bf16[6,24,256]{2,1,0:T(8,128)(2,1)S(1)}, u32[]{:S(2)}, u32[]{:S(2)}) collective-permute-start(bf16[6,24,256]{2,1,0:T(8,128)(2,1)S(1)} %get-tuple-element.16), channel_id=1, source_target_pairs={{0,1},{1,0},{2,3},{3,2},{4,5},{5,4},{6,7},{7,6},{8,9},{9,8},{10,11... | collective-permute-start | bytes 221192 | tf_op jit(solution)/shard_map/ppermute | solution.py:314
  17.7 4.3 %collective-permute-start.3 = (bf16[6,24,256]{2,1,0:T(8,128)(2,1)S(1)}, bf16[6,24,256]{2,1,0:T(8,128)(2,1)S(1)}, u32[]{:S(2)}, u32[]{:S(2)}) collective-permute-start(bf16[6,24,256]{2,1,0:T(8,128)(2,1)S(1)} %get-tuple-element.17), channel_id=1, source_target_pairs={{0,16},{1,17},{2,754},{3,755},{4,20},{5,21},{6,758},{7,759},{8,24}... | collective-permute-start | bytes 221192 | tf_op jit(solution)/shard_map/ppermute | solution.py:314
  22.5 18.9 %collective-permute-start.4 = (bf16[6,24,256]{2,1,0:T(8,128)(2,1)S(1)}, bf16[6,24,256]{2,1,0:T(8,128)(2,1)S(1)}, u32[]{:S(2)}, u32[]{:S(2)}) collective-permute-start(bf16[6,24,256]{2,1,0:T(8,128)(2,1)S(1)} %get-tuple-element.19), channel_id=1, source_target_pairs={{0,15},{1,17},{2,18},{3,19},{4,3},{5,21},{6,22},{7,23},{8,7},{9,25... | collective-permute-start | bytes 221192 | tf_op jit(solution)/shard_map/ppermute | solution.py:314
  24.6 16.9 %collective-permute-start.5 = (bf16[6,24,256]{2,1,0:T(8,128)(2,1)S(1)}, bf16[6,24,256]{2,1,0:T(8,128)(2,1)S(1)}, u32[]{:S(2)}, u32[]{:S(2)}) collective-permute-start(bf16[6,24,256]{2,1,0:T(8,128)(2,1)S(1)} %get-tuple-element.20), channel_id=1, source_target_pairs={{0,1},{1,2},{2,754},{3,4},{4,5},{5,6},{6,758},{7,8},{8,9},{9,10},{... | collective-permute-start | bytes 221192 | tf_op jit(solution)/shard_map/ppermute | solution.py:314
  31.6 9.8 %collective-permute-start.6 = (bf16[6,24,256]{2,1,0:T(8,128)(2,1)S(1)}, bf16[6,24,256]{2,1,0:T(8,128)(2,1)S(1)}, u32[]{:S(2)}, u32[]{:S(2)}) collective-permute-start(bf16[6,24,256]{2,1,0:T(8,128)(2,1)S(1)} %get-tuple-element.21), channel_id=1, source_target_pairs={{0,752},{1,0},{2,3},{3,2},{4,756},{5,4},{6,7},{7,6},{8,760},{9,8},... | collective-permute-start | bytes 221192 | tf_op jit(solution)/shard_map/ppermute | solution.py:314
  34.5 11.7 %collective-permute-start.7 = (bf16[6,24,256]{2,1,0:T(8,128)(2,1)S(1)}, bf16[6,24,256]{2,1,0:T(8,128)(2,1)S(1)}, u32[]{:S(2)}, u32[]{:S(2)}) collective-permute-start(bf16[6,24,256]{2,1,0:T(8,128)(2,1)S(1)} %get-tuple-element.22), channel_id=1, source_target_pairs={{0,16},{1,753},{2,1},{3,755},{4,20},{5,757},{6,5},{7,759},{8,24},{... | collective-permute-start | bytes 221192 | tf_op jit(solution)/shard_map/ppermute | solution.py:314
